TPU v7x, 128 devices: a whole 4x4x4 slice. The times are simulated.
128 devices in a mesh: rows: 16 (over x, z), cols: 8 (over y, core).
Axes of the slice: x: 4, y: 4, z: 4, core: 2. Of those that a mesh axis runs over, the one named last changes fastest.
Arguments:
- bag_index: int32 [2048, 128], P(('rows', 'cols')), may hold values from 0 to 1048575, as said below
- bag_length: int32 [2048, 4], P(('rows', 'cols')), may hold values from 1 to 32
- emb_tables: float32 [4, 1048576, 128], P(None, ('rows', 'cols')), may hold values from -0.6 to 0.6
- dense_feats: float32 [2048, 128], P(('rows', 'cols')), may hold values from -6 to 6
- w_dense: float32 [128, 1024], replicated, may hold values from -0.5 to 0.5
- w_pair: float32 [10, 1024], replicated, may hold values from -0.5 to 0.5
- top_bias: float32 [1024], replicated, may hold values from -3 to 3
Outputs:
- pooled: float32 [2048, 4, 128], P(('rows', 'cols'))
- top_hidden: float32 [2048, 1024], P(('rows', 'cols'))
Inputs may be any that keep to these rules, and one draw needn't show every extreme that they name: `bag_length`: slots at or past a bag's length are ignored, whatever they hold. `bag_index`: device d holds rows d * 8192 to (d + 1) * 8192 - 1 of every table; among the 2048 slots (live or not) of the samples of one device, at most 32 hold rows of any one device, and in every draw some device's rows receive exactly 32 slots from every device.
All inputs are finite; a program needn't handle non-finite values.
Results may differ from a plain program's by a relative error of at most 0.0001.
Values sent between devices are 32-bit elements; how exact they have to be, the bound alone decides.
A program may use at most 128 MiB of HBM per device.

v0:
```python
import functools

import jax
import jax.numpy as jnp
from jax import lax
from jax.experimental import pallas as pl
from jax.experimental.pallas import tpu as pltpu
from jax.sharding import PartitionSpec as P

MESH = pl.DeviceIdType.MESH
F32 = jnp.float32
BF16 = jnp.bfloat16
LAG = 3
LAG_Z = 4
CHUNKS = 8


def kernel(
    dims,
    index_ref,
    length_ref,
    table_hbm,
    dense_ref,
    wd_hbm,
    wp_ref,
    bias_ref,
    pooled_ref,
    hidden_ref,
    table,
    wd,
    hidden,
    outbox,
    inbox,
    ids,
    rows_buf,
    core_out,
    core_in,
    keep,
    plane_out,
    plane_in,
    z_out,
    z_in,
    table_sem,
    wd_sem,
    box_send,
    box_recv,
    ids_sem,
    core_send,
    core_recv,
    plane_send,
    plane_recv,
    z_send,
    z_recv,
):
    nr, nc, nx, local_rows, nt, slots_bag, cap = dims
    n = nr * nc
    ny = nc // 2
    np_ = nx * ny
    nz = nr // nx
    groups = nz * np_
    samples, lanes = index_ref.shape
    width = table.shape[1]
    bags = samples * nt
    total_rows = nt * local_rows
    r = lax.axis_index("rows")
    c = lax.axis_index("cols")
    me = r * nc + c
    z, x, y, k = r // nx, r % nx, c // 2, c % 2
    p = x * ny + y

    def at(d):
        return {"rows": d // nc, "cols": d % nc}

    def place(zz, pp, kk):
        return zz * nx + pp // ny, (pp % ny) * 2 + kk

    def flat(zz, pp, kk):
        rr, cc = place(zz, pp, kk)
        return rr * nc + cc

    barrier = pltpu.get_barrier_semaphore()

    def greet(i, carry):
        d = (me + i) % n
        pl.semaphore_signal(barrier, inc=1, device_id=at(d), device_id_type=MESH)
        return carry

    lax.fori_loop(1, n, greet, 0)

    part = total_rows // CHUNKS
    table_copies = [
        pltpu.make_async_copy(
            table_hbm.at[pl.ds(i * part, part)], table.at[pl.ds(i * part, part)], table_sem.at[i]
        )
        for i in range(CHUNKS)
    ]
    wd_copy = pltpu.make_async_copy(wd_hbm, wd, wd_sem)
    for copy in table_copies:
        copy.start()
    wd_copy.start()

    idx = index_ref[...]
    lane = lax.broadcasted_iota(jnp.int32, (samples, lanes), 1)
    table_of = lane // slots_bag
    length = jnp.zeros((samples, lanes), jnp.int32)
    for t in range(nt):
        length = jnp.where(table_of == t, length_ref[:, t : t + 1], length)
    live = lane - table_of * slots_bag < length
    if local_rows & (local_rows - 1) == 0:
        owner = lax.shift_right_logical(idx, jnp.full_like(idx, local_rows.bit_length() - 1))
    else:
        owner = idx // local_rows
    row = table_of * local_rows + idx - owner * local_rows
    bag = table_of * samples + lax.broadcasted_iota(jnp.int32, (samples, lanes), 0)
    owner = jnp.where(live, owner, -1)
    pieces = []
    shift = 0
    while shift == 0 or (total_rows - 1) >> shift:
        pieces.append((row // (1 << shift)) % 256)
        shift += 8
    n_row = len(pieces)
    shift = 0
    while shift == 0 or bags >> shift:
        pieces.append(((bag + 1) // (1 << shift)) % 256)
        shift += 8
    pieces = [v.astype(F32) for v in pieces]
    dev_iota = lax.broadcasted_iota(jnp.int32, (n, lanes), 0)
    before = (
        lax.broadcasted_iota(jnp.int32, (lanes, lanes), 0)
        < lax.broadcasted_iota(jnp.int32, (lanes, lanes), 1)
    )
    before = jnp.where(before, 1.0, 0.0).astype(BF16)
    hots = [
        jnp.where(owner[b : b + 1, :] == dev_iota, 1.0, 0.0).astype(F32) for b in range(samples)
    ]
    prefix = jnp.dot(
        jnp.concatenate([h.astype(BF16) for h in hots], axis=0), before, preferred_element_type=F32
    )
    base = jnp.zeros((n, 1), F32)
    box = jnp.zeros((len(pieces) * n, cap), F32)
    cap_iota = lax.broadcasted_iota(jnp.int32, (cap, lanes), 0)
    for b in range(samples):
        hot = hots[b]
        rank = jnp.sum(hot * (prefix[b * n : (b + 1) * n, :] + base), axis=0, keepdims=True)
        base = base + jnp.sum(hot, axis=1, keepdims=True)
        spot = jnp.where(rank.astype(jnp.int32) == cap_iota, 1.0, 0.0).astype(BF16)
        coded = jnp.concatenate([hot * v[b : b + 1, :] for v in pieces], axis=0).astype(BF16)
        box = box + lax.dot_general(
            coded, spot, (((1,), (1,)), ((), ())), preferred_element_type=F32
        )
    box_row = jnp.zeros((n, cap), jnp.int32)
    box_bag = jnp.full((n, cap), -1, jnp.int32)
    for i in range(len(pieces)):
        piece = box[i * n : (i + 1) * n, :].astype(jnp.int32)
        if i < n_row:
            box_row = box_row + piece * (1 << (8 * i))
        else:
            box_bag = box_bag + piece * (1 << (8 * (i - n_row)))
    for d in range(n):
        outbox[d, 0:1, :] = box_row[d : d + 1, :]
        outbox[d, 1:2, :] = box_bag[d : d + 1, :]
    inbox[me] = outbox[me]

    pl.semaphore_wait(barrier, n - 1)

    def box_copy(d, source):
        return pltpu.make_async_remote_copy(
            src_ref=outbox.at[d],
            dst_ref=inbox.at[source],
            send_sem=box_send.at[d],
            recv_sem=box_recv.at[source],
            device_id=at(d),
            device_id_type=MESH,
        )

    def send_box(i, carry):
        box_copy((me + i) % n, me).start()
        return carry

    lax.fori_loop(1, n, send_box, 0)

    wd_copy.wait()
    hidden[...] = (
        jnp.dot(
            dense_ref[...], wd[...], precision=lax.Precision.HIGHEST, preferred_element_type=F32
        )
        + bias_ref[...]
    )

    def ids_copy(d):
        return pltpu.make_async_copy(inbox.at[d], ids.at[d], ids_sem.at[d])

    ids_copy(me).start()

    def take_box(i, carry):
        d = (me + n - i) % n
        box_copy((me + i) % n, d).wait_recv()
        ids_copy(d).start()
        return carry

    lax.fori_loop(1, n, take_box, 0)
    for d in range(n):
        ids_copy(d).wait()
    for copy in table_copies:
        copy.wait()

    bag_iota = lax.broadcasted_iota(jnp.int32, (bags, cap), 0)

    def inside(at_row):
        if total_rows & (total_rows - 1) == 0:
            return at_row & (total_rows - 1)
        return jnp.clip(at_row, 0, total_rows - 1)

    def fetch(d, slot):
        for i in range(cap):
            rows_buf[slot, i : i + 1, :] = table[pl.ds(inside(ids[d, 0, i]), 1), :]

    def pool(d, slot):
        found = rows_buf[slot]
        high = found.astype(BF16)
        low = (found - high.astype(F32)).astype(BF16)
        select = jnp.where(inbox[d, 1:2, :] == bag_iota, 1.0, 0.0).astype(BF16)
        both = jnp.dot(select, jnp.concatenate([high, low], axis=1), preferred_element_type=F32)
        return both[:, :width] + both[:, width:]

    def target(j):
        return (z + 1 + j // np_) % nz, (p + 1 + j % np_) % np_

    def core_copy(g):
        return pltpu.make_async_remote_copy(
            src_ref=core_out.at[g],
            dst_ref=core_in.at[g],
            send_sem=core_send.at[g],
            recv_sem=core_recv.at[g],
            device_id={"rows": r, "cols": y * 2 + 1 - k},
            device_id_type=MESH,
        )

    def plane_copy(zz, pp, source):
        rr, cc = place(z, pp, k)
        return pltpu.make_async_remote_copy(
            src_ref=plane_out.at[zz * np_ + pp],
            dst_ref=plane_in.at[zz * np_ + source],
            send_sem=plane_send.at[zz * np_ + pp],
            recv_sem=plane_recv.at[zz * np_ + source],
            device_id={"rows": rr, "cols": cc},
            device_id_type=MESH,
        )

    def z_copy(zz, source):
        rr, cc = place(zz, p, k)
        return pltpu.make_async_remote_copy(
            src_ref=z_out.at[zz],
            dst_ref=z_in.at[source],
            send_sem=z_send.at[zz],
            recv_sem=z_recv.at[source],
            device_id={"rows": rr, "cols": cc},
            device_id_type=MESH,
        )

    def step(it, carry):
        @pl.when(it < groups)
        def _():
            zz, pp = target(it)
            g = zz * np_ + pp
            mate = flat(zz, pp, 1 - k)
            own = flat(zz, pp, k)
            fetch(mate, 0)
            core_out[g] = pool(mate, 0)
            fetch(own, 1)
            keep[g] = pool(own, 1)
            core_copy(g).start()

        j = it - LAG

        @pl.when((j >= 0) & (j < groups))
        def _():
            zz, pp = target(j)
            g = zz * np_ + pp
            core_copy(g).wait_recv()
            summed = core_in[g] + keep[g]

            @pl.when(j % np_ == np_ - 1)
            def _():
                plane_in[g] = summed

            @pl.when(j % np_ < np_ - 1)
            def _():
                plane_out[g] = summed
                plane_copy(zz, pp, p).start()

        h = it - LAG - LAG_Z

        @pl.when((h >= 0) & (h % np_ == np_ - 1))
        def _():
            zi = h // np_
            zz = (z + 1 + zi) % nz
            summed = plane_in[zz * np_ + p]
            for i in range(1, np_):
                other = (p + i) % np_
                plane_copy(zz, other, other).wait_recv()
                summed = summed + plane_in[zz * np_ + other]

            @pl.when(zi < nz - 1)
            def _():
                z_out[zz] = summed
                z_copy(zz, z).start()

            @pl.when(zi == nz - 1)
            def _():
                z_in[z] = summed

        return carry

    lax.fori_loop(0, groups + LAG + LAG_Z, step, 0)

    pooled = z_in[z]
    for i in range(1, nz):
        other = (z + i) % nz
        z_copy(other, other).wait_recv()
        pooled = pooled + z_in[other]

    feats = [dense_ref[...]]
    for t in range(nt):
        feats.append(pooled[t * samples : (t + 1) * samples, :])
        pooled_ref[:, t, :] = feats[-1]
    total = hidden[...]
    pair = 0
    for first in range(nt + 1):
        for second in range(first + 1, nt + 1):
            dots = jnp.sum(feats[first] * feats[second], axis=-1, keepdims=True)
            total = total + dots * wp_ref[pair : pair + 1, :]
            pair += 1
    hidden_ref[...] = jnp.maximum(total, 0.0)

    def drain_box(i, carry):
        box_copy((me + i) % n, me).wait_send()
        return carry

    lax.fori_loop(1, n, drain_box, 0)

    def drain(j, carry):
        zz, pp = target(j)
        core_copy(zz * np_ + pp).wait_send()

        @pl.when(j % np_ < np_ - 1)
        def _():
            plane_copy(zz, pp, p).wait_send()

        return carry

    lax.fori_loop(0, groups, drain, 0)
    for i in range(1, nz):
        z_copy((z + i) % nz, z).wait_send()


def shards(nr, nc, bag_index, bag_length, emb_tables, dense_feats, w_dense, w_pair, top_bias):
    samples, lanes = bag_index.shape
    nt, local_rows, width = emb_tables.shape
    n = nr * nc
    slots = samples * lanes
    cap = 2 * slots // n
    bags = samples * nt
    units = w_dense.shape[1]
    nx = 2 if nr % 2 == 0 else 1
    groups = n // 2
    nz = nr // nx
    dims = (nr, nc, nx, local_rows, nt, lanes // nt, cap)
    vmem = pl.BlockSpec(memory_space=pltpu.VMEM)
    anyw = pl.BlockSpec(memory_space=pl.ANY)
    blocks = lambda m: pltpu.VMEM((m, bags, width), F32)
    dma = pltpu.SemaphoreType.DMA
    pooled, hidden = pl.pallas_call(
        functools.partial(kernel, dims),
        out_shape=(
            jax.ShapeDtypeStruct((samples, nt, width), F32),
            jax.ShapeDtypeStruct((samples, units), F32),
        ),
        in_specs=[vmem, vmem, anyw, vmem, anyw, vmem, vmem],
        out_specs=(vmem, vmem),
        scratch_shapes=[
            pltpu.VMEM((nt * local_rows, width), F32),
            pltpu.VMEM(w_dense.shape, F32),
            pltpu.VMEM((samples, units), F32),
            pltpu.VMEM((n, 2, cap), jnp.int32),
            pltpu.VMEM((n, 2, cap), jnp.int32),
            pltpu.SMEM((n, 2, cap), jnp.int32),
            pltpu.VMEM((2, cap, width), F32),
            blocks(groups),
            blocks(groups),
            blocks(groups),
            blocks(groups),
            blocks(groups),
            blocks(nz),
            blocks(nz),
            dma((CHUNKS,)),
            dma,
            dma((n,)),
            dma((n,)),
            dma((n,)),
            dma((groups,)),
            dma((groups,)),
            dma((groups,)),
            dma((groups,)),
            dma((nz,)),
            dma((nz,)),
        ],
        compiler_params=pltpu.CompilerParams(
            collective_id=0, has_side_effects=True, vmem_limit_bytes=60 * 1024 * 1024
        ),
    )(
        bag_index,
        bag_length,
        emb_tables.reshape(nt * local_rows, width),
        dense_feats,
        w_dense,
        w_pair,
        top_bias.reshape(1, units),
    )
    return pooled, hidden


def solution(mesh):
    nr, nc = mesh.shape["rows"], mesh.shape["cols"]
    in_specs = (
        P(("rows", "cols"), None),
        P(("rows", "cols"), None),
        P(None, ("rows", "cols"), None),
        P(("rows", "cols"), None),
        P(),
        P(),
        P(),
    )
    out_specs = (P(("rows", "cols"), None, None), P(("rows", "cols"), None))
    return jax.shard_map(
        functools.partial(shards, nr, nc),
        mesh=mesh,
        in_specs=in_specs,
        out_specs=out_specs,
        check_vma=False,
    )
```

profile of v0, /device:TPU:0, one launch (start us, length us, event | category | flops | bytes accessed | tf_op | source)
XLA Modules:
  0.0 75.6 jit_solution(7951485751060416705)
XLA Ops:
  0.6 1.4 %copy.9.length_ref = s32[16,4]{1,0:T(8,128)} copy(s32[16,4]{0,1:T(4,128)} %param.8) | data formatting | bytes 512 | tf_op args[1]
  2.0 70.8 %shard_map.86 = (f32[16,4,128]{2,1,0:T(4,128)}, f32[16,1024]{1,0:T(8,128)}) custom-call(s32[16,128]{1,0:T(8,128)} %index_ref.1, s32[16,4]{1,0:T(8,128)} %copy.9.length_ref, f32[32768,128]{1,0:T(8,128)} %bitcast.2, f32[16,128]{1,0:T(8,128)} %dense_ref.1, f32[128,1024]{1,0:T(8,128)} %wd_hbm.1, f32[10,1024]{1,0:T(8,128)} %wp_ref.1, f32[1,1024]{1,0:T(1,128)} %bitcast.3), custom_call_target="tpu_custom_call" | custom-call | tf_op jit(solution)/shard_map/pallas_call | solution.py:373
  72.8 1.4 %copy.12 = f32[16,4,128]{2,1,0:T(4,128)} copy(f32[16,4,128]{2,1,0:T(4,128)} %get-tuple-element.4) | data formatting | bytes 65536
  74.2 1.5 %copy.13 = f32[16,1024]{1,0:T(8,128)} copy(f32[16,1024]{1,0:T(8,128)} %get-tuple-element.5) | data formatting | bytes 131072
where the time goes:
time: 76.2 us; the launch traced here: 75.6 us
  Pallas kernels  70.8 us (93%)
  local copies, waits for them, and re-layouts  4.2 us (6%)
    pallas_call x1, Pallas kernels, shards(): pl.pallas_call(functools.partial(kernel, dims), out_shape=(jax.ShapeDtype...  70.8 us
    unnamed x3, local copies, waits for them, and re-layouts  4.2 us

commit v1 on v0

v1 whole, which is shorter than its diff:
```python
import functools

import jax
import jax.numpy as jnp
from jax import lax
from jax.experimental import pallas as pl
from jax.experimental.pallas import tpu as pltpu
from jax.sharding import PartitionSpec as P

MESH = pl.DeviceIdType.MESH
F32 = jnp.float32
BF16 = jnp.bfloat16
I32 = jnp.int32
SIDE = 4
CHIPS = SIDE**3
CHUNKS = 8
LAG = 5
AHEAD = 3
CUT = (0, 24, 48, 64)


def kernel(
    dims,
    index_hbm,
    length_hbm,
    table_hbm,
    dense_hbm,
    wd_hbm,
    wp_hbm,
    bias_hbm,
    pooled_ref,
    hidden_ref,
    index_ref,
    length_ref,
    dense_ref,
    wp_ref,
    bias_ref,
    table,
    wd,
    hidden,
    outbox,
    inbox,
    matebox,
    ids_own,
    ids_mate,
    mate_out,
    rows_all,
    a_out,
    a_in,
    b_out,
    b_in,
    input_sem,
    table_sem,
    box_send,
    box_recv,
    fwd_send,
    fwd_recv,
    own_sem,
    mate_sem,
    rows_send,
    rows_recv,
    a_send,
    x_recv,
    y_recv,
    z_recv,
    b_send,
    b_recv,
):
    local_rows, nt, slots_bag, cap = dims
    n = 2 * CHIPS
    samples, lanes = index_ref.shape
    bags = samples * nt
    total_rows = nt * local_rows
    r = lax.axis_index("rows")
    c = lax.axis_index("cols")
    x, z, y, k = r // SIDE, r % SIDE, c // 2, c % 2

    def step_by(at, d):
        return (at + d) % SIDE

    def device(xx, yy, zz, kk):
        return {"rows": xx * SIDE + zz, "cols": yy * 2 + kk}

    offsets = [
        (dx, dy, dz) for dz in range(SIDE) for dy in range(SIDE) for dx in range(SIDE) if dx or dy or dz
    ]
    offsets.sort(key=lambda o: -sum(min(d, SIDE - d) for d in o))

    inputs = [
        pltpu.make_async_copy(source, target, input_sem.at[i])
        for i, (source, target) in enumerate(
            (
                (index_hbm, index_ref),
                (length_hbm, length_ref),
                (wd_hbm, wd),
                (dense_hbm, dense_ref),
                (wp_hbm, wp_ref),
                (bias_hbm, bias_ref),
            )
        )
    ]
    for copy in inputs[:2]:
        copy.start()

    barrier = pltpu.get_barrier_semaphore()
    for dx, dy, dz in offsets:
        pl.semaphore_signal(
            barrier,
            inc=1,
            device_id=device(step_by(x, dx), step_by(y, dy), step_by(z, dz), k),
            device_id_type=MESH,
        )
    mate = device(x, y, z, 1 - k)
    pl.semaphore_signal(barrier, inc=1, device_id=mate, device_id_type=MESH)

    inputs[0].wait()
    inputs[1].wait()
    for copy in inputs[2:]:
        copy.start()
    part = total_rows // CHUNKS
    for i in range(CHUNKS):
        pltpu.make_async_copy(
            table_hbm.at[pl.ds(i * part, part)], table.at[pl.ds(i * part, part)], table_sem
        ).start()

    idx = index_ref[...]
    lane = lax.broadcasted_iota(I32, (samples, lanes), 1)
    table_of = lane // slots_bag
    spread = jnp.where(
        lax.broadcasted_iota(I32, (nt, lanes), 1) // slots_bag == lax.broadcasted_iota(I32, (nt, lanes), 0),
        1.0,
        0.0,
    )
    length = lax.dot_general(
        length_ref[...].astype(F32).astype(BF16),
        spread.astype(BF16),
        (((0,), (0,)), ((), ())),
        preferred_element_type=F32,
    ).astype(I32)
    live = lane - table_of * slots_bag < length
    owner = idx // local_rows
    row = table_of * local_rows + idx - owner * local_rows
    bag = table_of * samples + lax.broadcasted_iota(I32, (samples, lanes), 0)
    owner = jnp.where(live, (owner % 2) * CHIPS + owner // 2, -1)
    pieces = []
    shift = 0
    while shift == 0 or (total_rows - 1) >> shift:
        pieces.append((row // (1 << shift)) % 256)
        shift += 8
    n_row = len(pieces)
    pieces.append(bag + 1)
    pieces = [v.astype(F32) for v in pieces]
    dev_iota = lax.broadcasted_iota(I32, (n, lanes), 0)
    before = (
        lax.broadcasted_iota(I32, (lanes, lanes), 0) < lax.broadcasted_iota(I32, (lanes, lanes), 1)
    )
    before = jnp.where(before, 1.0, 0.0).astype(BF16)
    hots = [
        jnp.where(owner[b : b + 1, :] == dev_iota, 1.0, 0.0).astype(F32) for b in range(samples)
    ]
    prefix = jnp.dot(
        jnp.concatenate([h.astype(BF16) for h in hots], axis=0), before, preferred_element_type=F32
    )
    base = jnp.zeros((n, 1), F32)
    box = jnp.zeros((len(pieces) * n, cap), F32)
    cap_iota = lax.broadcasted_iota(I32, (cap, lanes), 0)
    for b in range(samples):
        hot = hots[b]
        rank = jnp.sum(hot * (prefix[b * n : (b + 1) * n, :] + base), axis=0, keepdims=True)
        base = base + jnp.sum(hot, axis=1, keepdims=True)
        spot = jnp.where(rank.astype(I32) == cap_iota, 1.0, 0.0).astype(BF16)
        coded = jnp.concatenate([hot * v[b : b + 1, :] for v in pieces], axis=0).astype(BF16)
        box = box + lax.dot_general(
            coded, spot, (((1,), (1,)), ((), ())), preferred_element_type=F32
        )
    box_row = jnp.zeros((n, cap), I32)
    for i in range(n_row):
        box_row = box_row + box[i * n : (i + 1) * n, :].astype(I32) * (1 << (8 * i))
    box_bag = box[n_row * n :, :].astype(I32) - 1
    flip = jnp.full((CHIPS, cap), k, I32) == 1
    halves = []
    for both in (box_bag, box_row):
        halves.append(jnp.where(flip, both[CHIPS:], both[:CHIPS]))
        halves.append(jnp.where(flip, both[:CHIPS], both[CHIPS:]))
    boxes = jnp.concatenate(halves, axis=1)
    for d in range(CHIPS):
        outbox[d] = boxes[d : d + 1, :]

    def chip(xx, yy, zz):
        return (xx * SIDE + zz) * SIDE + yy

    inbox[CHIPS - 1] = outbox[chip(x, y, z)]

    pl.semaphore_wait(barrier, CHIPS)

    def slot_of(dx, dy, dz):
        return ((dz - 1) % SIDE * SIDE + (dy - 1) % SIDE) * SIDE + (dx - 1) % SIDE

    for dx, dy, dz in offsets:
        xx, yy, zz = step_by(x, SIDE - dx), step_by(y, SIDE - dy), step_by(z, SIDE - dz)
        pltpu.make_async_remote_copy(
            src_ref=outbox.at[chip(xx, yy, zz)],
            dst_ref=inbox.at[slot_of(dx, dy, dz)],
            send_sem=box_send,
            recv_sem=box_recv,
            device_id=device(xx, yy, zz, k),
            device_id_type=MESH,
        ).start()

    for copy in inputs[2:]:
        copy.wait()
    hidden[...] = (
        jnp.dot(
            dense_ref[...], wd[...], precision=lax.Precision.HIGHEST, preferred_element_type=F32
        )
        + bias_ref[...]
    )

    rest = pl.ds(0, CHIPS - 1)
    boxes_moved = pltpu.make_async_remote_copy(
        src_ref=outbox.at[rest],
        dst_ref=inbox.at[rest],
        send_sem=box_send,
        recv_sem=box_recv,
        device_id=mate,
        device_id_type=MESH,
    )
    boxes_moved.wait_recv()
    forward = pltpu.make_async_remote_copy(
        src_ref=inbox,
        dst_ref=matebox,
        send_sem=fwd_send,
        recv_sem=fwd_recv,
        device_id=mate,
        device_id_type=MESH,
    )
    forward.start()
    own_copy = pltpu.make_async_copy(inbox, ids_own, own_sem)
    own_copy.start()
    forward.wait_recv()

    def mate_copy(q):
        some = pl.ds(q * (CHIPS // SIDE), CHIPS // SIDE)
        return pltpu.make_async_copy(matebox.at[some], ids_mate.at[some], mate_sem.at[q])

    for q in range(SIDE):
        mate_copy(q).start()
    pltpu.make_async_copy(table_hbm, table, table_sem).wait()
    own_copy.wait()

    def inside(at):
        return at & (total_rows - 1)

    def rows_copy(s):
        some = pl.ds(s * SIDE, SIDE)
        return pltpu.make_async_remote_copy(
            src_ref=mate_out.at[some],
            dst_ref=rows_all.at[some, pl.ds(cap, cap)],
            send_sem=rows_send,
            recv_sem=rows_recv.at[s],
            device_id=mate,
            device_id_type=MESH,
        )

    def fetch_mate(s):
        for u in range(SIDE):
            t = s * SIDE + u
            for i in range(cap):
                mate_out[t, i : i + 1, :] = table[pl.ds(inside(ids_mate[t, 0, 3 * cap + i]), 1), :]
        rows_copy(s).start()

    bag_iota = lax.broadcasted_iota(I32, (bags, 2 * cap), 0)

    def a_copy(t, p, to, recv):
        rows = pl.ds(CUT[p], CUT[p + 1] - CUT[p])
        return pltpu.make_async_remote_copy(
            src_ref=a_out.at[t, rows],
            dst_ref=a_in.at[t, rows],
            send_sem=a_send,
            recv_sem=recv,
            device_id=to,
            device_id_type=MESH,
        )

    def b_copy(g, p, to):
        rows = pl.ds(CUT[p], CUT[p + 1] - CUT[p])
        return pltpu.make_async_remote_copy(
            src_ref=b_out.at[g, rows],
            dst_ref=b_in.at[g, rows],
            send_sem=b_send,
            recv_sem=b_recv,
            device_id=to,
            device_id_type=MESH,
        )

    def arrived(slots, p, sem):
        rows = pl.ds(CUT[p], CUT[p + 1] - CUT[p])
        pltpu.make_async_remote_copy(
            src_ref=a_in.at[slots, rows],
            dst_ref=a_in.at[slots, rows],
            send_sem=a_send,
            recv_sem=sem,
            device_id=mate,
            device_id_type=MESH,
        ).wait_recv()

    def pass_on(g, p, slots, to, last):
        lo, hi = CUT[p], CUT[p + 1]
        total = a_in[slots[0], lo:hi, :]
        for t in slots[1:]:
            total = total + a_in[t, lo:hi, :]
        if last is None:
            b_out[g, lo:hi, :] = total
            b_copy(g, p, to).start()
            return

        @pl.when(jnp.logical_not(last))
        def _():
            b_out[g, lo:hi, :] = total
            b_copy(g, p, to).start()

        @pl.when(last)
        def _():
            b_in[g, lo:hi, :] = total

    groups = CHIPS // SIDE

    def step(it, carry):
        @pl.when(it < groups)
        def _():
            @pl.when(it % SIDE == 0)
            def _():
                mate_copy(it // SIDE).wait()

            fetch_mate(it)

        s = it - AHEAD

        @pl.when((s >= 0) & (s < groups))
        def _():
            v, w = s % SIDE, s // SIDE
            rows_copy(s).wait_recv()
            yy, zz = step_by(y, v + 1), step_by(z, w + 1)
            for u in range(SIDE):
                t = s * SIDE + u
                for i in range(cap):
                    rows_all[t, i : i + 1, :] = table[pl.ds(inside(ids_own[t, 0, 2 * cap + i]), 1), :]
            for u in range(SIDE):
                t = s * SIDE + u
                found = rows_all[t]
                high = found.astype(BF16)
                low = (found - high.astype(F32)).astype(BF16)
                select = jnp.where(inbox[t, 0:1, 0 : 2 * cap] == bag_iota, 1.0, 0.0).astype(BF16)
                a_out[t] = jnp.dot(select, high, preferred_element_type=F32) + jnp.dot(
                    select, low, preferred_element_type=F32
                )
            for u in range(SIDE):
                t = s * SIDE + u
                if u < SIDE - 1:
                    a_copy(t, 0, device(step_by(x, u + 1), y, z, k), x_recv.at[s]).start()
                else:
                    a_in[t, CUT[0] : CUT[1], :] = a_out[t, CUT[0] : CUT[1], :]

            @pl.when(v < SIDE - 1)
            def _():
                for u in range(SIDE):
                    a_copy(s * SIDE + u, 1, device(x, yy, z, k), y_recv.at[w]).start()

            @pl.when(v == SIDE - 1)
            def _():
                for u in range(SIDE):
                    t = s * SIDE + u
                    a_in[t, CUT[1] : CUT[2], :] = a_out[t, CUT[1] : CUT[2], :]

            @pl.when(w < SIDE - 1)
            def _():
                for u in range(SIDE):
                    a_copy(s * SIDE + u, 2, device(x, y, zz, k), z_recv).start()

            @pl.when(w == SIDE - 1)
            def _():
                for u in range(SIDE):
                    t = s * SIDE + u
                    a_in[t, CUT[2] : CUT[3], :] = a_out[t, CUT[2] : CUT[3], :]

        j = s - LAG

        @pl.when(j >= 0)
        def _():
            arrived(pl.ds(j * SIDE, SIDE - 1), 0, x_recv.at[j])
            to = device(x, step_by(y, j % SIDE + 1), step_by(z, j // SIDE + 1), k)
            pass_on(j, 0, [j * SIDE + u for u in range(SIDE)], to, j == groups - 1)

        @pl.when((j >= 0) & (j % SIDE == SIDE - 1))
        def _():
            w = j // SIDE
            arrived(pl.ds(w * groups, groups - SIDE), 1, y_recv.at[w])
            for u in range(SIDE):
                to = device(step_by(x, u + 1), y, step_by(z, w + 1), k)
                slots = [w * groups + v * SIDE + u for v in range(SIDE)]
                pass_on(w * SIDE + u, 1, slots, to, w == SIDE - 1 if u == SIDE - 1 else None)

        @pl.when(j == groups - SIDE)
        def _():
            arrived(pl.ds(0, CHIPS - groups), 2, z_recv)

        @pl.when(j >= groups - SIDE)
        def _():
            v = j - (groups - SIDE)
            for u in range(SIDE):
                to = device(step_by(x, u + 1), step_by(y, v + 1), z, k)
                slots = [w * groups + v * SIDE + u for w in range(SIDE)]
                pass_on(v * SIDE + u, 2, slots, to, v == SIDE - 1 if u == SIDE - 1 else None)

        return carry

    lax.fori_loop(0, groups + AHEAD + LAG, step, 0)

    some = pl.ds(0, groups - 1)
    b_moved = pltpu.make_async_remote_copy(
        src_ref=b_out.at[some],
        dst_ref=b_in.at[some],
        send_sem=b_send,
        recv_sem=b_recv,
        device_id=mate,
        device_id_type=MESH,
    )
    b_moved.wait_recv()
    pooled = b_in[0]
    for g in range(1, groups):
        pooled = pooled + b_in[g]

    feats = [dense_ref[...]]
    for t in range(nt):
        feats.append(pooled[t * samples : (t + 1) * samples, :])
        pooled_ref[:, t, :] = feats[-1]
    total = hidden[...]
    pair = 0
    for one in range(nt + 1):
        for two in range(one + 1, nt + 1):
            dots = jnp.sum(feats[one] * feats[two], axis=-1, keepdims=True)
            total = total + dots * wp_ref[pair : pair + 1, :]
            pair += 1
    hidden_ref[...] = jnp.maximum(total, 0.0)

    boxes_moved.wait_send()
    forward.wait_send()
    pltpu.make_async_remote_copy(
        src_ref=mate_out,
        dst_ref=mate_out,
        send_sem=rows_send,
        recv_sem=b_recv,
        device_id=mate,
        device_id_type=MESH,
    ).wait_send()
    some = pl.ds(0, CHIPS - groups)
    pltpu.make_async_remote_copy(
        src_ref=a_out.at[some],
        dst_ref=a_in.at[some],
        send_sem=a_send,
        recv_sem=b_recv,
        device_id=mate,
        device_id_type=MESH,
    ).wait_send()
    b_moved.wait_send()


def shards(bag_index, bag_length, emb_tables, dense_feats, w_dense, w_pair, top_bias):
    samples, lanes = bag_index.shape
    nt, local_rows, width = emb_tables.shape
    cap = 2 * samples * lanes // (2 * CHIPS)
    bags = samples * nt
    units = w_dense.shape[1]
    groups = CHIPS // SIDE
    dims = (local_rows, nt, lanes // nt, cap)
    vmem = pl.BlockSpec(memory_space=pltpu.VMEM)
    anyw = pl.BlockSpec(memory_space=pl.ANY)
    dma = pltpu.SemaphoreType.DMA
    return pl.pallas_call(
        functools.partial(kernel, dims),
        out_shape=(
            jax.ShapeDtypeStruct((samples, nt, width), F32),
            jax.ShapeDtypeStruct((samples, units), F32),
        ),
        in_specs=[anyw] * 7,
        out_specs=(vmem, vmem),
        scratch_shapes=[
            pltpu.VMEM((samples, lanes), I32),
            pltpu.VMEM((nt, samples), I32),
            pltpu.VMEM((samples, width), F32),
            pltpu.VMEM(w_pair.shape, F32),
            pltpu.VMEM((1, units), F32),
            pltpu.VMEM((nt * local_rows, width), F32),
            pltpu.VMEM(w_dense.shape, F32),
            pltpu.VMEM((samples, units), F32),
            pltpu.VMEM((CHIPS, 1, 4 * cap), I32),
            pltpu.VMEM((CHIPS, 1, 4 * cap), I32),
            pltpu.VMEM((CHIPS, 1, 4 * cap), I32),
            pltpu.SMEM((CHIPS, 1, 4 * cap), I32),
            pltpu.SMEM((CHIPS, 1, 4 * cap), I32),
            pltpu.VMEM((CHIPS, cap, width), F32),
            pltpu.VMEM((CHIPS, 2 * cap, width), F32),
            pltpu.VMEM((CHIPS, bags, width), F32),
            pltpu.VMEM((CHIPS, bags, width), F32),
            pltpu.VMEM((groups, bags, width), F32),
            pltpu.VMEM((groups, bags, width), F32),
            dma((6,)),
            dma,
            dma,
            dma,
            dma,
            dma,
            dma,
            dma((SIDE,)),
            dma,
            dma((groups,)),
            dma,
            dma((groups,)),
            dma((SIDE,)),
            dma,
            dma,
            dma,
        ],
        compiler_params=pltpu.CompilerParams(
            collective_id=0, has_side_effects=True, vmem_limit_bytes=60 * 1024 * 1024
        ),
    )(
        bag_index,
        bag_length.T,
        emb_tables.reshape(nt * local_rows, width),
        dense_feats,
        w_dense,
        w_pair,
        top_bias.reshape(1, units),
    )


def solution(mesh):
    in_specs = (
        P(("rows", "cols"), None),
        P(("rows", "cols"), None),
        P(None, ("rows", "cols"), None),
        P(("rows", "cols"), None),
        P(),
        P(),
        P(),
    )
    out_specs = (P(("rows", "cols"), None, None), P(("rows", "cols"), None))
    return jax.shard_map(
        shards, mesh=mesh, in_specs=in_specs, out_specs=out_specs, check_vma=False
    )
```

time: 76.2 us -> 41.2 us (0.54)
  the two profiles are of different devices: /device:TPU:0 before, /device:TPU:32 now
where the time goes in v1:
time: 41.2 us; the launch traced here: 41 us
  Pallas kernels  37.5 us (91%)
  local copies, waits for them, and re-layouts  2.85 us (7%)
  between operations  0.64 us (2%)
    pallas_call x1, Pallas kernels, shards(): pl.pallas_call(functools.partial(kernel, dims), out_shape=(jax.ShapeDtype...  37.5 us
    unnamed x2, local copies, waits for them, and re-layouts  2.85 us

profile of v1, /device:TPU:32, one launch (start us, length us, event | category | flops | bytes accessed | tf_op | source)
XLA Modules:
  0.0 41.0 jit_solution(8150046866239528885)
XLA Ops:
  0.6 37.5 %shard_map.86 = (f32[16,4,128]{2,1,0:T(4,128)}, f32[16,1024]{1,0:T(8,128)}) custom-call(s32[16,128]{1,0:T(8,128)} %index_hbm.1, s32[4,16]{1,0:T(4,128)} %bitcast.5, f32[32768,128]{1,0:T(8,128)} %bitcast.3, f32[16,128]{1,0:T(8,128)} %dense_hbm.1, f32[128,1024]{1,0:T(8,128)} %wd_hbm.1, f32[10,1024]{1,0:T(8,128)} %wp_hbm.1, f32[1,1024]{1,0:T(1,128)} %bitcast.4), custom_call_target="tpu_custom_call" | custom-call | tf_op jit(solution)/shard_map/pallas_call | solution.py:479
  38.1 1.4 %copy.11 = f32[16,4,128]{2,1,0:T(4,128)} copy(f32[16,4,128]{2,1,0:T(4,128)} %get-tuple-element.4) | data formatting | bytes 65536
  39.5 1.5 %copy.12 = f32[16,1024]{1,0:T(8,128)} copy(f32[16,1024]{1,0:T(8,128)} %get-tuple-element.5) | data formatting | bytes 131072

commit v2 on v1

--- a/solution.py
+++ b/solution.py
@@ -14,8 +14,8 @@
 SIDE = 4
 CHIPS = SIDE**3
 CHUNKS = 8
-LAG = 5
-AHEAD = 3
+AHEAD = 5
+Z_AT = 9
 CUT = (0, 24, 48, 64)
 
 
@@ -26,25 +26,24 @@
     table_hbm,
     dense_hbm,
     wd_hbm,
-    wp_hbm,
     bias_hbm,
-    pooled_ref,
-    hidden_ref,
+    sums_ref,
+    start_ref,
     index_ref,
     length_ref,
     dense_ref,
-    wp_ref,
     bias_ref,
     table,
     wd,
-    hidden,
     outbox,
     inbox,
+    want,
     matebox,
     ids_own,
     ids_mate,
     mate_out,
-    rows_all,
+    own_rows,
+    mate_rows,
     a_out,
     a_in,
     b_out,
@@ -86,6 +85,9 @@
     ]
     offsets.sort(key=lambda o: -sum(min(d, SIDE - d) for d in o))
 
+    def far_first(v):
+        return (2 + 3 * v + 3 * (v * (v - 1) // 2)) % SIDE
+
     inputs = [
         pltpu.make_async_copy(source, target, input_sem.at[i])
         for i, (source, target) in enumerate(
@@ -94,7 +96,6 @@
                 (length_hbm, length_ref),
                 (wd_hbm, wd),
                 (dense_hbm, dense_ref),
-                (wp_hbm, wp_ref),
                 (bias_hbm, bias_ref),
             )
         )
@@ -194,7 +195,8 @@
     pl.semaphore_wait(barrier, CHIPS)
 
     def slot_of(dx, dy, dz):
-        return ((dz - 1) % SIDE * SIDE + (dy - 1) % SIDE) * SIDE + (dx - 1) % SIDE
+        place = [far_first(v) for v in range(SIDE)]
+        return (place.index(dz) * SIDE + place.index(dy)) * SIDE + place.index(dx)
 
     for dx, dy, dz in offsets:
         xx, yy, zz = step_by(x, SIDE - dx), step_by(y, SIDE - dy), step_by(z, SIDE - dz)
@@ -209,7 +211,7 @@
 
     for copy in inputs[2:]:
         copy.wait()
-    hidden[...] = (
+    start_ref[...] = (
         jnp.dot(
             dense_ref[...], wd[...], precision=lax.Precision.HIGHEST, preferred_element_type=F32
         )
@@ -226,8 +228,9 @@
         device_id_type=MESH,
     )
     boxes_moved.wait_recv()
+    want[...] = inbox[...] & (total_rows - 1)
     forward = pltpu.make_async_remote_copy(
-        src_ref=inbox,
+        src_ref=want,
         dst_ref=matebox,
         send_sem=fwd_send,
         recv_sem=fwd_recv,
@@ -235,7 +238,7 @@
         device_id_type=MESH,
     )
     forward.start()
-    own_copy = pltpu.make_async_copy(inbox, ids_own, own_sem)
+    own_copy = pltpu.make_async_copy(want, ids_own, own_sem)
     own_copy.start()
     forward.wait_recv()
 
@@ -248,14 +251,11 @@
     pltpu.make_async_copy(table_hbm, table, table_sem).wait()
     own_copy.wait()
 
-    def inside(at):
-        return at & (total_rows - 1)
-
     def rows_copy(s):
         some = pl.ds(s * SIDE, SIDE)
         return pltpu.make_async_remote_copy(
             src_ref=mate_out.at[some],
-            dst_ref=rows_all.at[some, pl.ds(cap, cap)],
+            dst_ref=mate_rows.at[some],
             send_sem=rows_send,
             recv_sem=rows_recv.at[s],
             device_id=mate,
@@ -266,16 +266,30 @@
         for u in range(SIDE):
             t = s * SIDE + u
             for i in range(cap):
-                mate_out[t, i : i + 1, :] = table[pl.ds(inside(ids_mate[t, 0, 3 * cap + i]), 1), :]
+                mate_out[t, i : i + 1, :] = table[pl.ds(ids_mate[t, 0, 3 * cap + i], 1), :]
         rows_copy(s).start()
 
+    def fetch_own(s):
+        for u in range(SIDE):
+            t = s * SIDE + u
+            for i in range(cap):
+                own_rows[u, i : i + 1, :] = table[pl.ds(ids_own[t, 0, 2 * cap + i], 1), :]
+
+    for s in range(AHEAD):
+        if s % SIDE == 0:
+            mate_copy(s // SIDE).wait()
+        fetch_mate(s)
+    fetch_own(0)
+    for q in range((AHEAD + SIDE - 1) // SIDE, SIDE):
+        mate_copy(q).wait()
+
     bag_iota = lax.broadcasted_iota(I32, (bags, 2 * cap), 0)
 
-    def a_copy(t, p, to, recv):
+    def a_copy(slots, p, to, recv):
         rows = pl.ds(CUT[p], CUT[p + 1] - CUT[p])
         return pltpu.make_async_remote_copy(
-            src_ref=a_out.at[t, rows],
-            dst_ref=a_in.at[t, rows],
+            src_ref=a_out.at[slots, rows],
+            dst_ref=a_in.at[slots, rows],
             send_sem=a_send,
             recv_sem=recv,
             device_id=to,
@@ -325,96 +339,93 @@
 
     groups = CHIPS // SIDE
 
-    def step(it, carry):
-        @pl.when(it < groups)
-        def _():
-            @pl.when(it % SIDE == 0)
-            def _():
-                mate_copy(it // SIDE).wait()
-
-            fetch_mate(it)
-
-        s = it - AHEAD
-
-        @pl.when((s >= 0) & (s < groups))
-        def _():
-            v, w = s % SIDE, s // SIDE
-            rows_copy(s).wait_recv()
-            yy, zz = step_by(y, v + 1), step_by(z, w + 1)
+    def keep_own(s, p):
+        lo, hi = CUT[p], CUT[p + 1]
+        for u in range(SIDE):
+            t = s * SIDE + u
+            a_in[t, lo:hi, :] = a_out[t, lo:hi, :]
+
+    def pool(s, more):
+        v, w = s % SIDE, s // SIDE
+        rows_copy(s).wait_recv()
+        for u in range(SIDE):
+            t = s * SIDE + u
+            found = jnp.concatenate([own_rows[u], mate_rows[t]], axis=0)
+            high = found.astype(BF16)
+            low = (found - high.astype(F32)).astype(BF16)
+            select = jnp.where(want[t, 0:1, 0 : 2 * cap] == bag_iota, 1.0, 0.0).astype(BF16)
+            value = jnp.dot(select, high, preferred_element_type=F32) + jnp.dot(
+                select, low, preferred_element_type=F32
+            )
+            a_out[t] = value
+            if u == SIDE - 1:
+                a_in[t, CUT[0] : CUT[1], :] = value[CUT[0] : CUT[1]]
+        if more:
+            fetch_own(s + 1)
+            fetch_mate(s + AHEAD)
+        else:
+            fetch_own(jnp.minimum(s + 1, groups - 1))
+        for u in range(SIDE - 1):
+            to = device(step_by(x, far_first(u)), y, z, k)
+            a_copy(pl.ds(s * SIDE + u, 1), 0, to, x_recv.at[s]).start()
+        four = pl.ds(s * SIDE, SIDE)
+
+        @pl.when(v < SIDE - 1)
+        def _():
+            a_copy(four, 1, device(x, step_by(y, far_first(v)), z, k), y_recv.at[w]).start()
+
+        @pl.when(w < SIDE - 1)
+        def _():
+            a_copy(four, 2, device(x, y, step_by(z, far_first(w)), k), z_recv).start()
+
+        @pl.when(v == SIDE - 1)
+        def _():
+            keep_own(s, 1)
+
+        @pl.when(w == SIDE - 1)
+        def _():
+            keep_own(s, 2)
+
+    def reduce(j, carry):
+        i = j - Z_AT
+
+        @pl.when(i == 0)
+        def _():
+            arrived(pl.ds(0, CHIPS - groups), 2, z_recv)
+
+        @pl.when((i >= 0) & (i < SIDE))
+        def _():
             for u in range(SIDE):
-                t = s * SIDE + u
-                for i in range(cap):
-                    rows_all[t, i : i + 1, :] = table[pl.ds(inside(ids_own[t, 0, 2 * cap + i]), 1), :]
-            for u in range(SIDE):
-                t = s * SIDE + u
-                found = rows_all[t]
-                high = found.astype(BF16)
-                low = (found - high.astype(F32)).astype(BF16)
-                select = jnp.where(inbox[t, 0:1, 0 : 2 * cap] == bag_iota, 1.0, 0.0).astype(BF16)
-                a_out[t] = jnp.dot(select, high, preferred_element_type=F32) + jnp.dot(
-                    select, low, preferred_element_type=F32
-                )
-            for u in range(SIDE):
-                t = s * SIDE + u
-                if u < SIDE - 1:
-                    a_copy(t, 0, device(step_by(x, u + 1), y, z, k), x_recv.at[s]).start()
-                else:
-                    a_in[t, CUT[0] : CUT[1], :] = a_out[t, CUT[0] : CUT[1], :]
-
-            @pl.when(v < SIDE - 1)
-            def _():
-                for u in range(SIDE):
-                    a_copy(s * SIDE + u, 1, device(x, yy, z, k), y_recv.at[w]).start()
-
-            @pl.when(v == SIDE - 1)
-            def _():
-                for u in range(SIDE):
-                    t = s * SIDE + u
-                    a_in[t, CUT[1] : CUT[2], :] = a_out[t, CUT[1] : CUT[2], :]
-
-            @pl.when(w < SIDE - 1)
-            def _():
-                for u in range(SIDE):
-                    a_copy(s * SIDE + u, 2, device(x, y, zz, k), z_recv).start()
-
-            @pl.when(w == SIDE - 1)
-            def _():
-                for u in range(SIDE):
-                    t = s * SIDE + u
-                    a_in[t, CUT[2] : CUT[3], :] = a_out[t, CUT[2] : CUT[3], :]
-
-        j = s - LAG
-
-        @pl.when(j >= 0)
-        def _():
-            arrived(pl.ds(j * SIDE, SIDE - 1), 0, x_recv.at[j])
-            to = device(x, step_by(y, j % SIDE + 1), step_by(z, j // SIDE + 1), k)
-            pass_on(j, 0, [j * SIDE + u for u in range(SIDE)], to, j == groups - 1)
-
-        @pl.when((j >= 0) & (j % SIDE == SIDE - 1))
+                to = device(step_by(x, far_first(u)), step_by(y, far_first(i)), z, k)
+                slots = [w * groups + i * SIDE + u for w in range(SIDE)]
+                pass_on(i * SIDE + u, 2, slots, to, i == SIDE - 1 if u == SIDE - 1 else None)
+
+        arrived(pl.ds(j * SIDE, SIDE - 1), 0, x_recv.at[j])
+        to = device(x, step_by(y, far_first(j % SIDE)), step_by(z, far_first(j // SIDE)), k)
+        pass_on(j, 0, [j * SIDE + u for u in range(SIDE)], to, j == groups - 1)
+
+        @pl.when(j % SIDE == SIDE - 1)
         def _():
             w = j // SIDE
             arrived(pl.ds(w * groups, groups - SIDE), 1, y_recv.at[w])
             for u in range(SIDE):
-                to = device(step_by(x, u + 1), y, step_by(z, w + 1), k)
+                to = device(step_by(x, far_first(u)), y, step_by(z, far_first(w)), k)
                 slots = [w * groups + v * SIDE + u for v in range(SIDE)]
                 pass_on(w * SIDE + u, 1, slots, to, w == SIDE - 1 if u == SIDE - 1 else None)
 
-        @pl.when(j == groups - SIDE)
-        def _():
-            arrived(pl.ds(0, CHIPS - groups), 2, z_recv)
-
-        @pl.when(j >= groups - SIDE)
-        def _():
-            v = j - (groups - SIDE)
-            for u in range(SIDE):
-                to = device(step_by(x, u + 1), step_by(y, v + 1), z, k)
-                slots = [w * groups + v * SIDE + u for w in range(SIDE)]
-                pass_on(v * SIDE + u, 2, slots, to, v == SIDE - 1 if u == SIDE - 1 else None)
-
         return carry
 
-    lax.fori_loop(0, groups + AHEAD + LAG, step, 0)
+    def step_full(s, carry):
+        pool(s, True)
+        return carry
+
+    def step_last(s, carry):
+        pool(s, False)
+        return carry
+
+    lax.fori_loop(0, groups - AHEAD, step_full, 0)
+    lax.fori_loop(groups - AHEAD, groups, step_last, 0)
+    lax.fori_loop(0, groups, reduce, 0)
 
     some = pl.ds(0, groups - 1)
     b_moved = pltpu.make_async_remote_copy(
@@ -430,18 +441,7 @@
     for g in range(1, groups):
         pooled = pooled + b_in[g]
 
-    feats = [dense_ref[...]]
-    for t in range(nt):
-        feats.append(pooled[t * samples : (t + 1) * samples, :])
-        pooled_ref[:, t, :] = feats[-1]
-    total = hidden[...]
-    pair = 0
-    for one in range(nt + 1):
-        for two in range(one + 1, nt + 1):
-            dots = jnp.sum(feats[one] * feats[two], axis=-1, keepdims=True)
-            total = total + dots * wp_ref[pair : pair + 1, :]
-            pair += 1
-    hidden_ref[...] = jnp.maximum(total, 0.0)
+    sums_ref[...] = pooled
 
     boxes_moved.wait_send()
     forward.wait_send()
@@ -465,6 +465,23 @@
     b_moved.wait_send()
 
 
+def interact(sums_ref, start_ref, dense_ref, wp_ref, pooled_ref, hidden_ref):
+    samples, nt = pooled_ref.shape[0], pooled_ref.shape[1]
+    pooled = sums_ref[...]
+    feats = [dense_ref[...]]
+    for t in range(nt):
+        feats.append(pooled[t * samples : (t + 1) * samples, :])
+        pooled_ref[:, t, :] = feats[-1]
+    total = start_ref[...]
+    pair = 0
+    for one in range(nt + 1):
+        for two in range(one + 1, nt + 1):
+            dots = jnp.sum(feats[one] * feats[two], axis=-1, keepdims=True)
+            total = total + dots * wp_ref[pair : pair + 1, :]
+            pair += 1
+    hidden_ref[...] = jnp.maximum(total, 0.0)
+
+
 def shards(bag_index, bag_length, emb_tables, dense_feats, w_dense, w_pair, top_bias):
     samples, lanes = bag_index.shape
     nt, local_rows, width = emb_tables.shape
@@ -476,35 +493,35 @@
     vmem = pl.BlockSpec(memory_space=pltpu.VMEM)
     anyw = pl.BlockSpec(memory_space=pl.ANY)
     dma = pltpu.SemaphoreType.DMA
-    return pl.pallas_call(
+    sums, start = pl.pallas_call(
         functools.partial(kernel, dims),
         out_shape=(
-            jax.ShapeDtypeStruct((samples, nt, width), F32),
+            jax.ShapeDtypeStruct((bags, width), F32),
             jax.ShapeDtypeStruct((samples, units), F32),
         ),
-        in_specs=[anyw] * 7,
+        in_specs=[anyw] * 6,
         out_specs=(vmem, vmem),
         scratch_shapes=[
             pltpu.VMEM((samples, lanes), I32),
             pltpu.VMEM((nt, samples), I32),
             pltpu.VMEM((samples, width), F32),
-            pltpu.VMEM(w_pair.shape, F32),
             pltpu.VMEM((1, units), F32),
             pltpu.VMEM((nt * local_rows, width), F32),
             pltpu.VMEM(w_dense.shape, F32),
-            pltpu.VMEM((samples, units), F32),
+            pltpu.VMEM((CHIPS, 1, 4 * cap), I32),
             pltpu.VMEM((CHIPS, 1, 4 * cap), I32),
             pltpu.VMEM((CHIPS, 1, 4 * cap), I32),
             pltpu.VMEM((CHIPS, 1, 4 * cap), I32),
             pltpu.SMEM((CHIPS, 1, 4 * cap), I32),
             pltpu.SMEM((CHIPS, 1, 4 * cap), I32),
             pltpu.VMEM((CHIPS, cap, width), F32),
-            pltpu.VMEM((CHIPS, 2 * cap, width), F32),
+            pltpu.VMEM((SIDE, cap, width), F32),
+            pltpu.VMEM((CHIPS, cap, width), F32),
             pltpu.VMEM((CHIPS, bags, width), F32),
             pltpu.VMEM((CHIPS, bags, width), F32),
             pltpu.VMEM((groups, bags, width), F32),
             pltpu.VMEM((groups, bags, width), F32),
-            dma((6,)),
+            dma((5,)),
             dma,
             dma,
             dma,
@@ -530,9 +547,17 @@
         emb_tables.reshape(nt * local_rows, width),
         dense_feats,
         w_dense,
-        w_pair,
         top_bias.reshape(1, units),
     )
+    return pl.pallas_call(
+        interact,
+        out_shape=(
+            jax.ShapeDtypeStruct((samples, nt, width), F32),
+            jax.ShapeDtypeStruct((samples, units), F32),
+        ),
+        in_specs=[vmem] * 4,
+        out_specs=(vmem, vmem),
+    )(sums, start, dense_feats, w_pair)
 
 
 def solution(mesh):

time: 41.2 us -> 37.1 us (0.900)
  the two profiles are of different devices: /device:TPU:32 before, /device:TPU:0 now
where the time goes in v2:
time: 37.1 us; the launch traced here: 36.9 us
  Pallas kernels  36.3 us (98%)
  between operations  0.64 us (2%)
    pallas_call x1, Pallas kernels, shards(): pl.pallas_call(functools.partial(kernel, dims), out_shape=(jax.ShapeDtype...  34.6 us
    pallas_call x1, Pallas kernels, shards(): pl.pallas_call(interact, out_shape=(jax.ShapeDtypeStruct((samples, nt, wi...  1.68 us

profile of v2, /device:TPU:0, one launch (start us, length us, event | category | flops | bytes accessed | tf_op | source)
XLA Modules:
  0.0 36.9 jit_solution(2851239571702329302)
XLA Ops:
  0.6 34.6 %shard_map.86 = (f32[64,128]{1,0:T(8,128)}, f32[16,1024]{1,0:T(8,128)}) custom-call(s32[16,128]{1,0:T(8,128)} %index_hbm.1, s32[4,16]{1,0:T(4,128)} %bitcast.5, f32[32768,128]{1,0:T(8,128)} %bitcast.3, f32[16,128]{1,0:T(8,128)} %dense_ref.1, f32[128,1024]{1,0:T(8,128)} %wd_hbm.1, f32[1,1024]{1,0:T(1,128)} %bitcast.4), custom_call_target="tpu_custom_call" | custom-call | tf_op jit(solution)/shard_map/pallas_call | solution.py:496
  35.2 1.7 %shard_map.87 = (f32[16,4,128]{2,1,0:T(4,128)}, f32[16,1024]{1,0:T(8,128)}) custom-call(f32[64,128]{1,0:T(8,128)} %get-tuple-element.4.sums_ref, f32[16,1024]{1,0:T(8,128)} %get-tuple-element.5.start_ref, f32[16,128]{1,0:T(8,128)} %dense_ref.1, f32[10,1024]{1,0:T(8,128)} %wp_ref.1), custom_call_target="tpu_custom_call" | custom-call | tf_op jit(solution)/shard_map/pallas_call | solution.py:552

commit v3 on v2

--- a/solution.py
+++ b/solution.py
@@ -15,8 +15,45 @@
 CHIPS = SIDE**3
 CHUNKS = 8
 AHEAD = 5
-Z_AT = 9
 CUT = (0, 24, 48, 64)
+FAR = SIDE // 2
+
+
+def destinations():
+    near = [1, 3, 0]
+    out = []
+    for far in ((1, 1, 1), (1, 1, 0), (1, 0, 1), (0, 1, 1), (1, 0, 0), (0, 1, 0), (0, 0, 1), (0, 0, 0)):
+        dims = [[FAR] if f else near for f in far]
+        out += [(dx, dy, dz) for dz in dims[2] for dy in dims[1] for dx in dims[0]]
+    return out
+
+
+ORDER = destinations()
+SLOT = {d: t for t, d in enumerate(ORDER)}
+
+
+def others(d, p):
+    return tuple(v for q, v in enumerate(d) if q != p)
+
+
+def along(p, v, o):
+    return o[:p] + (v,) + o[p:]
+
+
+def plane_order():
+    near = [1, 3, 0]
+    out = [(FAR, FAR)] + [(FAR, b) for b in near] + [(a, FAR) for a in near]
+    return out + [(a, b) for b in near for a in near]
+
+
+PLANE = plane_order()
+PLACE = {o: g for g, o in enumerate(PLANE)}
+TEAM = [0] * 7 + [1] * 3 + [2] * 3 + [3] * 3
+TEAMS = 4
+
+
+def joined(o):
+    return 1 if sum(o) % 2 == 0 else SIDE - 1
 
 
 def kernel(
@@ -39,6 +76,7 @@
     inbox,
     want,
     matebox,
+    mate_want,
     ids_own,
     ids_mate,
     mate_out,
@@ -59,9 +97,8 @@
     rows_send,
     rows_recv,
     a_send,
-    x_recv,
-    y_recv,
-    z_recv,
+    far_recv,
+    near_recv,
     b_send,
     b_recv,
 ):
@@ -80,13 +117,10 @@
     def device(xx, yy, zz, kk):
         return {"rows": xx * SIDE + zz, "cols": yy * 2 + kk}
 
-    offsets = [
-        (dx, dy, dz) for dz in range(SIDE) for dy in range(SIDE) for dx in range(SIDE) if dx or dy or dz
-    ]
-    offsets.sort(key=lambda o: -sum(min(d, SIDE - d) for d in o))
-
-    def far_first(v):
-        return (2 + 3 * v + 3 * (v * (v - 1) // 2)) % SIDE
+    offsets = sorted(ORDER, key=lambda o: -sum(min(d, SIDE - d) for d in o))
+
+    def shifted(d, kk):
+        return device(step_by(x, d[0]), step_by(y, d[1]), step_by(z, d[2]), kk)
 
     inputs = [
         pltpu.make_async_copy(source, target, input_sem.at[i])
@@ -103,16 +137,13 @@
     for copy in inputs[:2]:
         copy.start()
 
+    mate = device(x, y, z, 1 - k)
+
     barrier = pltpu.get_barrier_semaphore()
-    for dx, dy, dz in offsets:
-        pl.semaphore_signal(
-            barrier,
-            inc=1,
-            device_id=device(step_by(x, dx), step_by(y, dy), step_by(z, dz), k),
-            device_id_type=MESH,
-        )
-    mate = device(x, y, z, 1 - k)
-    pl.semaphore_signal(barrier, inc=1, device_id=mate, device_id_type=MESH)
+    for d in offsets:
+        pl.semaphore_signal(barrier, inc=1, device_id=shifted(d, 1 - k), device_id_type=MESH)
+        if any(d):
+            pl.semaphore_signal(barrier, inc=1, device_id=shifted(d, k), device_id_type=MESH)
 
     inputs[0].wait()
     inputs[1].wait()
@@ -190,24 +221,30 @@
     def chip(xx, yy, zz):
         return (xx * SIDE + zz) * SIDE + yy
 
-    inbox[CHIPS - 1] = outbox[chip(x, y, z)]
-
-    pl.semaphore_wait(barrier, CHIPS)
-
-    def slot_of(dx, dy, dz):
-        place = [far_first(v) for v in range(SIDE)]
-        return (place.index(dz) * SIDE + place.index(dy)) * SIDE + place.index(dx)
-
-    for dx, dy, dz in offsets:
-        xx, yy, zz = step_by(x, SIDE - dx), step_by(y, SIDE - dy), step_by(z, SIDE - dz)
+    inbox[SLOT[(0, 0, 0)]] = outbox[chip(x, y, z)]
+
+    pl.semaphore_wait(barrier, n - 1)
+
+    for d in offsets:
+        back = tuple((SIDE - v) % SIDE for v in d)
+        source = outbox.at[chip(step_by(x, back[0]), step_by(y, back[1]), step_by(z, back[2]))]
         pltpu.make_async_remote_copy(
-            src_ref=outbox.at[chip(xx, yy, zz)],
-            dst_ref=inbox.at[slot_of(dx, dy, dz)],
-            send_sem=box_send,
-            recv_sem=box_recv,
-            device_id=device(xx, yy, zz, k),
+            src_ref=source,
+            dst_ref=matebox.at[SLOT[d]],
+            send_sem=fwd_send,
+            recv_sem=fwd_recv,
+            device_id=shifted(back, 1 - k),
             device_id_type=MESH,
         ).start()
+        if any(d):
+            pltpu.make_async_remote_copy(
+                src_ref=source,
+                dst_ref=inbox.at[SLOT[d]],
+                send_sem=box_send,
+                recv_sem=box_recv,
+                device_id=shifted(back, k),
+                device_id_type=MESH,
+            ).start()
 
     for copy in inputs[2:]:
         copy.wait()
@@ -227,29 +264,29 @@
         device_id=mate,
         device_id_type=MESH,
     )
-    boxes_moved.wait_recv()
-    want[...] = inbox[...] & (total_rows - 1)
-    forward = pltpu.make_async_remote_copy(
-        src_ref=want,
+    mates_moved = pltpu.make_async_remote_copy(
+        src_ref=outbox,
         dst_ref=matebox,
         send_sem=fwd_send,
         recv_sem=fwd_recv,
         device_id=mate,
         device_id_type=MESH,
     )
-    forward.start()
+    quarter = CHIPS // SIDE
+
+    def mate_copy(q):
+        some = pl.ds(q * quarter, quarter)
+        return pltpu.make_async_copy(mate_want.at[some], ids_mate.at[some], mate_sem.at[q])
+
+    mates_moved.wait_recv()
+    mate_want[...] = matebox[...] & (total_rows - 1)
+    for q in range(SIDE):
+        mate_copy(q).start()
+    boxes_moved.wait_recv()
+    want[...] = inbox[...] & (total_rows - 1)
     own_copy = pltpu.make_async_copy(want, ids_own, own_sem)
     own_copy.start()
-    forward.wait_recv()
-
-    def mate_copy(q):
-        some = pl.ds(q * (CHIPS // SIDE), CHIPS // SIDE)
-        return pltpu.make_async_copy(matebox.at[some], ids_mate.at[some], mate_sem.at[q])
-
-    for q in range(SIDE):
-        mate_copy(q).start()
     pltpu.make_async_copy(table_hbm, table, table_sem).wait()
-    own_copy.wait()
 
     def rows_copy(s):
         some = pl.ds(s * SIDE, SIDE)
@@ -279,78 +316,53 @@
         if s % SIDE == 0:
             mate_copy(s // SIDE).wait()
         fetch_mate(s)
+    own_copy.wait()
     fetch_own(0)
     for q in range((AHEAD + SIDE - 1) // SIDE, SIDE):
         mate_copy(q).wait()
 
     bag_iota = lax.broadcasted_iota(I32, (bags, 2 * cap), 0)
 
-    def a_copy(slots, p, to, recv):
-        rows = pl.ds(CUT[p], CUT[p + 1] - CUT[p])
+    def rows_of(p):
+        return pl.ds(CUT[p], CUT[p + 1] - CUT[p])
+
+    def a_copy(t, p, shift, recv):
         return pltpu.make_async_remote_copy(
-            src_ref=a_out.at[slots, rows],
-            dst_ref=a_in.at[slots, rows],
+            src_ref=a_out.at[t, rows_of(p)],
+            dst_ref=a_in.at[t, rows_of(p)],
             send_sem=a_send,
             recv_sem=recv,
-            device_id=to,
+            device_id=shifted(along(p, shift, (0, 0)), k),
             device_id_type=MESH,
         )
 
-    def b_copy(g, p, to):
-        rows = pl.ds(CUT[p], CUT[p + 1] - CUT[p])
+    def b_copy(g, p):
         return pltpu.make_async_remote_copy(
-            src_ref=b_out.at[g, rows],
-            dst_ref=b_in.at[g, rows],
+            src_ref=b_out.at[g, rows_of(p)],
+            dst_ref=b_in.at[g, rows_of(p)],
             send_sem=b_send,
             recv_sem=b_recv,
-            device_id=to,
+            device_id=shifted(along(p, 0, PLANE[g]), k),
             device_id_type=MESH,
         )
 
-    def arrived(slots, p, sem):
-        rows = pl.ds(CUT[p], CUT[p + 1] - CUT[p])
+    def arrived(count, p, sem):
         pltpu.make_async_remote_copy(
-            src_ref=a_in.at[slots, rows],
-            dst_ref=a_in.at[slots, rows],
+            src_ref=a_in.at[pl.ds(0, count), rows_of(p)],
+            dst_ref=a_in.at[pl.ds(0, count), rows_of(p)],
             send_sem=a_send,
             recv_sem=sem,
             device_id=mate,
             device_id_type=MESH,
         ).wait_recv()
 
-    def pass_on(g, p, slots, to, last):
-        lo, hi = CUT[p], CUT[p + 1]
-        total = a_in[slots[0], lo:hi, :]
-        for t in slots[1:]:
-            total = total + a_in[t, lo:hi, :]
-        if last is None:
-            b_out[g, lo:hi, :] = total
-            b_copy(g, p, to).start()
-            return
-
-        @pl.when(jnp.logical_not(last))
-        def _():
-            b_out[g, lo:hi, :] = total
-            b_copy(g, p, to).start()
-
-        @pl.when(last)
-        def _():
-            b_in[g, lo:hi, :] = total
-
     groups = CHIPS // SIDE
 
-    def keep_own(s, p):
-        lo, hi = CUT[p], CUT[p + 1]
-        for u in range(SIDE):
-            t = s * SIDE + u
-            a_in[t, lo:hi, :] = a_out[t, lo:hi, :]
-
-    def pool(s, more):
-        v, w = s % SIDE, s // SIDE
+    def pool(s):
         rows_copy(s).wait_recv()
-        for u in range(SIDE):
-            t = s * SIDE + u
-            found = jnp.concatenate([own_rows[u], mate_rows[t]], axis=0)
+        slots = range(s * SIDE, (s + 1) * SIDE)
+        for t in slots:
+            found = jnp.concatenate([own_rows[t % SIDE], mate_rows[t]], axis=0)
             high = found.astype(BF16)
             low = (found - high.astype(F32)).astype(BF16)
             select = jnp.where(want[t, 0:1, 0 : 2 * cap] == bag_iota, 1.0, 0.0).astype(BF16)
@@ -358,74 +370,48 @@
                 select, low, preferred_element_type=F32
             )
             a_out[t] = value
-            if u == SIDE - 1:
-                a_in[t, CUT[0] : CUT[1], :] = value[CUT[0] : CUT[1]]
-        if more:
+            for p in range(3):
+                if ORDER[t][p] == 0:
+                    a_in[t, CUT[p] : CUT[p + 1], :] = value[CUT[p] : CUT[p + 1]]
+        if s + 1 < groups:
             fetch_own(s + 1)
+        if s + AHEAD < groups:
             fetch_mate(s + AHEAD)
-        else:
-            fetch_own(jnp.minimum(s + 1, groups - 1))
-        for u in range(SIDE - 1):
-            to = device(step_by(x, far_first(u)), y, z, k)
-            a_copy(pl.ds(s * SIDE + u, 1), 0, to, x_recv.at[s]).start()
-        four = pl.ds(s * SIDE, SIDE)
-
-        @pl.when(v < SIDE - 1)
-        def _():
-            a_copy(four, 1, device(x, step_by(y, far_first(v)), z, k), y_recv.at[w]).start()
-
-        @pl.when(w < SIDE - 1)
-        def _():
-            a_copy(four, 2, device(x, y, step_by(z, far_first(w)), k), z_recv).start()
-
-        @pl.when(v == SIDE - 1)
-        def _():
-            keep_own(s, 1)
-
-        @pl.when(w == SIDE - 1)
-        def _():
-            keep_own(s, 2)
-
-    def reduce(j, carry):
-        i = j - Z_AT
-
-        @pl.when(i == 0)
-        def _():
-            arrived(pl.ds(0, CHIPS - groups), 2, z_recv)
-
-        @pl.when((i >= 0) & (i < SIDE))
-        def _():
-            for u in range(SIDE):
-                to = device(step_by(x, far_first(u)), step_by(y, far_first(i)), z, k)
-                slots = [w * groups + i * SIDE + u for w in range(SIDE)]
-                pass_on(i * SIDE + u, 2, slots, to, i == SIDE - 1 if u == SIDE - 1 else None)
-
-        arrived(pl.ds(j * SIDE, SIDE - 1), 0, x_recv.at[j])
-        to = device(x, step_by(y, far_first(j % SIDE)), step_by(z, far_first(j // SIDE)), k)
-        pass_on(j, 0, [j * SIDE + u for u in range(SIDE)], to, j == groups - 1)
-
-        @pl.when(j % SIDE == SIDE - 1)
-        def _():
-            w = j // SIDE
-            arrived(pl.ds(w * groups, groups - SIDE), 1, y_recv.at[w])
-            for u in range(SIDE):
-                to = device(step_by(x, far_first(u)), y, step_by(z, far_first(w)), k)
-                slots = [w * groups + v * SIDE + u for v in range(SIDE)]
-                pass_on(w * SIDE + u, 1, slots, to, w == SIDE - 1 if u == SIDE - 1 else None)
-
-        return carry
-
-    def step_full(s, carry):
-        pool(s, True)
-        return carry
-
-    def step_last(s, carry):
-        pool(s, False)
-        return carry
-
-    lax.fori_loop(0, groups - AHEAD, step_full, 0)
-    lax.fori_loop(groups - AHEAD, groups, step_last, 0)
-    lax.fori_loop(0, groups, reduce, 0)
+        for t in slots:
+            for p in range(3):
+                o, v = others(ORDER[t], p), ORDER[t][p]
+                team = TEAM[PLACE[o]]
+                if v == FAR:
+                    a_copy(t, p, joined(o), far_recv.at[p, team]).start()
+                elif v and v != joined(o):
+                    a_copy(t, p, v, near_recv.at[p, team]).start()
+
+    for s in range(groups):
+        pool(s)
+    for team in range(TEAMS):
+        planes = [o for o in PLANE if TEAM[PLACE[o]] == team]
+        for p in range(3):
+            lo, hi = CUT[p], CUT[p + 1]
+            arrived(len(planes), p, far_recv.at[p, team])
+            for o in planes:
+                t, far = SLOT[along(p, joined(o), o)], SLOT[along(p, FAR, o)]
+                a_out[t, lo:hi, :] = a_out[t, lo:hi, :] + a_in[far, lo:hi, :]
+                a_copy(t, p, joined(o), near_recv.at[p, team]).start()
+    for team in range(TEAMS):
+        planes = [o for o in PLANE if TEAM[PLACE[o]] == team]
+        for p in range(3):
+            lo, hi = CUT[p], CUT[p + 1]
+            arrived(2 * len(planes), p, near_recv.at[p, team])
+            for o in planes:
+                g = PLACE[o]
+                total = a_in[SLOT[along(p, 0, o)], lo:hi, :]
+                for v in (1, SIDE - 1):
+                    total = total + a_in[SLOT[along(p, v, o)], lo:hi, :]
+                if any(o):
+                    b_out[g, lo:hi, :] = total
+                    b_copy(g, p).start()
+                else:
+                    b_in[g, lo:hi, :] = total
 
     some = pl.ds(0, groups - 1)
     b_moved = pltpu.make_async_remote_copy(
@@ -444,7 +430,7 @@
     sums_ref[...] = pooled
 
     boxes_moved.wait_send()
-    forward.wait_send()
+    mates_moved.wait_send()
     pltpu.make_async_remote_copy(
         src_ref=mate_out,
         dst_ref=mate_out,
@@ -512,6 +498,7 @@
             pltpu.VMEM((CHIPS, 1, 4 * cap), I32),
             pltpu.VMEM((CHIPS, 1, 4 * cap), I32),
             pltpu.VMEM((CHIPS, 1, 4 * cap), I32),
+            pltpu.VMEM((CHIPS, 1, 4 * cap), I32),
             pltpu.SMEM((CHIPS, 1, 4 * cap), I32),
             pltpu.SMEM((CHIPS, 1, 4 * cap), I32),
             pltpu.VMEM((CHIPS, cap, width), F32),
@@ -532,9 +519,8 @@
             dma,
             dma((groups,)),
             dma,
-            dma((groups,)),
-            dma((SIDE,)),
-            dma,
+            dma((3, TEAMS)),
+            dma((3, TEAMS)),
             dma,
             dma,
         ],

time: 37.1 us -> 34.8 us (0.938)
  Pallas kernels: 36.3 us -> 34 us
    pallas_call x1, Pallas kernels: 34.6 us -> 32.3 us  [shards(): pl.pallas_call(functools.partial(kernel, dims), out_shape=(jax.ShapeDtype...]
where the time goes in v3:
time: 34.8 us; the launch traced here: 34.6 us
  Pallas kernels  34 us (98%)
  between operations  0.64 us (2%)
    pallas_call x1, Pallas kernels, shards(): pl.pallas_call(functools.partial(kernel, dims), out_shape=(jax.ShapeDtype...  32.3 us
    pallas_call x1, Pallas kernels, shards(): pl.pallas_call(interact, out_shape=(jax.ShapeDtypeStruct((samples, nt, wi...  1.68 us

profile of v3, /device:TPU:0, one launch (start us, length us, event | category | flops | bytes accessed | tf_op | source)
XLA Modules:
  0.0 34.6 jit_solution(10444843277249565860)
XLA Ops:
  0.6 32.3 %shard_map.86 = (f32[64,128]{1,0:T(8,128)}, f32[16,1024]{1,0:T(8,128)}) custom-call(s32[16,128]{1,0:T(8,128)} %index_hbm.1, s32[4,16]{1,0:T(4,128)} %bitcast.5, f32[32768,128]{1,0:T(8,128)} %bitcast.3, f32[16,128]{1,0:T(8,128)} %dense_ref.1, f32[128,1024]{1,0:T(8,128)} %wd_hbm.1, f32[1,1024]{1,0:T(1,128)} %bitcast.4), custom_call_target="tpu_custom_call" | custom-call | tf_op jit(solution)/shard_map/pallas_call | solution.py:482
  32.9 1.7 %shard_map.87 = (f32[16,4,128]{2,1,0:T(4,128)}, f32[16,1024]{1,0:T(8,128)}) custom-call(f32[64,128]{1,0:T(8,128)} %get-tuple-element.4.sums_ref, f32[16,1024]{1,0:T(8,128)} %get-tuple-element.5.start_ref, f32[16,128]{1,0:T(8,128)} %dense_ref.1, f32[10,1024]{1,0:T(8,128)} %wp_ref.1), custom_call_target="tpu_custom_call" | custom-call | tf_op jit(solution)/shard_map/pallas_call | solution.py:538

commit v4 on v3

--- a/solution.py
+++ b/solution.py
@@ -74,9 +74,6 @@
     wd,
     outbox,
     inbox,
-    want,
-    matebox,
-    mate_want,
     ids_own,
     ids_mate,
     mate_out,
@@ -93,7 +90,6 @@
     fwd_send,
     fwd_recv,
     own_sem,
-    mate_sem,
     rows_send,
     rows_recv,
     a_send,
@@ -214,7 +210,7 @@
     for both in (box_bag, box_row):
         halves.append(jnp.where(flip, both[CHIPS:], both[:CHIPS]))
         halves.append(jnp.where(flip, both[:CHIPS], both[CHIPS:]))
-    boxes = jnp.concatenate(halves, axis=1)
+    boxes = jnp.concatenate(halves, axis=1) & (total_rows - 1)
     for d in range(CHIPS):
         outbox[d] = boxes[d : d + 1, :]
 
@@ -230,7 +226,7 @@
         source = outbox.at[chip(step_by(x, back[0]), step_by(y, back[1]), step_by(z, back[2]))]
         pltpu.make_async_remote_copy(
             src_ref=source,
-            dst_ref=matebox.at[SLOT[d]],
+            dst_ref=ids_mate.at[SLOT[d]],
             send_sem=fwd_send,
             recv_sem=fwd_recv,
             device_id=shifted(back, 1 - k),
@@ -266,7 +262,7 @@
     )
     mates_moved = pltpu.make_async_remote_copy(
         src_ref=outbox,
-        dst_ref=matebox,
+        dst_ref=ids_mate,
         send_sem=fwd_send,
         recv_sem=fwd_recv,
         device_id=mate,
@@ -274,18 +270,14 @@
     )
     quarter = CHIPS // SIDE
 
-    def mate_copy(q):
+    def own_copy(q):
         some = pl.ds(q * quarter, quarter)
-        return pltpu.make_async_copy(mate_want.at[some], ids_mate.at[some], mate_sem.at[q])
-
+        return pltpu.make_async_copy(inbox.at[some], ids_own.at[some], own_sem.at[q])
+
+    boxes_moved.wait_recv()
+    for q in range(SIDE):
+        own_copy(q).start()
     mates_moved.wait_recv()
-    mate_want[...] = matebox[...] & (total_rows - 1)
-    for q in range(SIDE):
-        mate_copy(q).start()
-    boxes_moved.wait_recv()
-    want[...] = inbox[...] & (total_rows - 1)
-    own_copy = pltpu.make_async_copy(want, ids_own, own_sem)
-    own_copy.start()
     pltpu.make_async_copy(table_hbm, table, table_sem).wait()
 
     def rows_copy(s):
@@ -313,13 +305,10 @@
                 own_rows[u, i : i + 1, :] = table[pl.ds(ids_own[t, 0, 2 * cap + i], 1), :]
 
     for s in range(AHEAD):
-        if s % SIDE == 0:
-            mate_copy(s // SIDE).wait()
         fetch_mate(s)
-    own_copy.wait()
+    for q in range(SIDE):
+        own_copy(q).wait()
     fetch_own(0)
-    for q in range((AHEAD + SIDE - 1) // SIDE, SIDE):
-        mate_copy(q).wait()
 
     bag_iota = lax.broadcasted_iota(I32, (bags, 2 * cap), 0)
 
@@ -365,7 +354,7 @@
             found = jnp.concatenate([own_rows[t % SIDE], mate_rows[t]], axis=0)
             high = found.astype(BF16)
             low = (found - high.astype(F32)).astype(BF16)
-            select = jnp.where(want[t, 0:1, 0 : 2 * cap] == bag_iota, 1.0, 0.0).astype(BF16)
+            select = jnp.where(inbox[t, 0:1, 0 : 2 * cap] == bag_iota, 1.0, 0.0).astype(BF16)
             value = jnp.dot(select, high, preferred_element_type=F32) + jnp.dot(
                 select, low, preferred_element_type=F32
             )
@@ -477,7 +466,7 @@
     groups = CHIPS // SIDE
     dims = (local_rows, nt, lanes // nt, cap)
     vmem = pl.BlockSpec(memory_space=pltpu.VMEM)
-    anyw = pl.BlockSpec(memory_space=pl.ANY)
+    anyw = pl.BlockSpec(memory_space=pltpu.HBM)
     dma = pltpu.SemaphoreType.DMA
     sums, start = pl.pallas_call(
         functools.partial(kernel, dims),
@@ -496,9 +485,6 @@
             pltpu.VMEM(w_dense.shape, F32),
             pltpu.VMEM((CHIPS, 1, 4 * cap), I32),
             pltpu.VMEM((CHIPS, 1, 4 * cap), I32),
-            pltpu.VMEM((CHIPS, 1, 4 * cap), I32),
-            pltpu.VMEM((CHIPS, 1, 4 * cap), I32),
-            pltpu.VMEM((CHIPS, 1, 4 * cap), I32),
             pltpu.SMEM((CHIPS, 1, 4 * cap), I32),
             pltpu.SMEM((CHIPS, 1, 4 * cap), I32),
             pltpu.VMEM((CHIPS, cap, width), F32),
@@ -514,7 +500,6 @@
             dma,
             dma,
             dma,
-            dma,
             dma((SIDE,)),
             dma,
             dma((groups,)),
@@ -525,15 +510,20 @@
             dma,
         ],
         compiler_params=pltpu.CompilerParams(
-            collective_id=0, has_side_effects=True, vmem_limit_bytes=60 * 1024 * 1024
+            collective_id=0, has_side_effects=True, vmem_limit_bytes=40 * 1024 * 1024
         ),
     )(
-        bag_index,
-        bag_length.T,
-        emb_tables.reshape(nt * local_rows, width),
-        dense_feats,
-        w_dense,
-        top_bias.reshape(1, units),
+        *(
+            pltpu.with_memory_space_constraint(v, pltpu.HBM)
+            for v in (
+                bag_index,
+                bag_length.T,
+                emb_tables.reshape(nt * local_rows, width),
+                dense_feats,
+                w_dense,
+                top_bias.reshape(1, units),
+            )
+        )
     )
     return pl.pallas_call(
         interact,
@@ -543,6 +533,7 @@
         ),
         in_specs=[vmem] * 4,
         out_specs=(vmem, vmem),
+        compiler_params=pltpu.CompilerParams(vmem_limit_bytes=8 * 1024 * 1024),
     )(sums, start, dense_feats, w_pair)
 
 

time: 34.8 us -> 33.1 us (0.951)
  Pallas kernels: 34 us -> 32.3 us
    pallas_call x1, Pallas kernels: 1.68 us -> 0.77 us  [shards(): pl.pallas_call(interact, out_shape=(jax.ShapeDtypeStruct((samples, nt, wi...]
    pallas_call x1, Pallas kernels: 32.3 us -> 31.5 us  [shards(): pl.pallas_call(functools.partial(kernel, dims), out_shape=(jax.ShapeDtype...]
where the time goes in v4:
time: 33.1 us; the launch traced here: 33 us
  Pallas kernels  32.3 us (98%)
  between operations  0.67 us (2%)
    pallas_call x1, Pallas kernels, shards(): pl.pallas_call(functools.partial(kernel, dims), out_shape=(jax.ShapeDtype...  31.5 us
    pallas_call x1, Pallas kernels, shards(): pl.pallas_call(interact, out_shape=(jax.ShapeDtypeStruct((samples, nt, wi...  0.77 us

profile of v4, /device:TPU:0, one launch (start us, length us, event | category | flops | bytes accessed | tf_op | source)
XLA Modules:
  0.0 33.0 jit_solution(12653514737936538442)
XLA Ops:
  0.6 0.0 copy-start.1
  0.6 0.0 copy-start
  0.7 31.5 %shard_map.86 = (f32[64,128]{1,0:T(8,128)S(1)}, f32[16,1024]{1,0:T(8,128)S(1)}) custom-call(s32[16,128]{1,0:T(8,128)} %index_hbm.1, s32[4,16]{1,0:T(4,128)} %bitcast.5, f32[32768,128]{1,0:T(8,128)} %bitcast.3, f32[16,128]{1,0:T(8,128)} %dense_ref.1, f32[128,1024]{1,0:T(8,128)} %wd_hbm.1, f32[1,1024]{1,0:T(1,128)} %bitcast.4), custom_call_target="tpu_custom_call" | custom-call | tf_op jit(solution)/shard_map/pallas_call | solution.py:471
  32.2 0.0 copy-done.1
  32.2 0.0 copy-done
  32.2 0.8 %shard_map.87 = (f32[16,4,128]{2,1,0:T(4,128)}, f32[16,1024]{1,0:T(8,128)}) custom-call(f32[64,128]{1,0:T(8,128)S(1)} %get-tuple-element.4.sums_ref, f32[16,1024]{1,0:T(8,128)S(1)} %get-tuple-element.5.start_ref, f32[16,128]{1,0:T(8,128)S(1)} %copy-done.1, f32[10,1024]{1,0:T(8,128)S(1)} %copy-done), custom_call_target="tpu_custom_call" | custom-call | tf_op jit(solution)/shard_map/pallas_call | solution.py:528
Async XLA Ops:
  0.6 31.5 %copy-start.1 = (f32[16,128]{1,0:T(8,128)S(1)}, f32[16,128]{1,0:T(8,128)}, u32[]{:S(2)}) copy-start(f32[16,128]{1,0:T(8,128)} %dense_ref.1) | copy-start | bytes 24580
  0.6 31.5 %copy-start = (f32[10,1024]{1,0:T(8,128)S(1)}, f32[10,1024]{1,0:T(8,128)}, u32[]{:S(2)}) copy-start(f32[10,1024]{1,0:T(8,128)} %wp_ref.1) | copy-start | bytes 122884

commit v5 on v4

--- a/solution.py
+++ b/solution.py
@@ -48,8 +48,9 @@
 
 PLANE = plane_order()
 PLACE = {o: g for g, o in enumerate(PLANE)}
-TEAM = [0] * 7 + [1] * 3 + [2] * 3 + [3] * 3
-TEAMS = 4
+TEAM = [0] * 4 + [1] * 3 + [2] * 3 + [3] * 3 + [4] * 3
+TEAMS = 5
+EARLY = {13: 0, 15: 1}
 
 
 def joined(o):
@@ -268,15 +269,10 @@
         device_id=mate,
         device_id_type=MESH,
     )
-    quarter = CHIPS // SIDE
-
-    def own_copy(q):
-        some = pl.ds(q * quarter, quarter)
-        return pltpu.make_async_copy(inbox.at[some], ids_own.at[some], own_sem.at[q])
-
+
+    own_copy = pltpu.make_async_copy(inbox, ids_own, own_sem)
     boxes_moved.wait_recv()
-    for q in range(SIDE):
-        own_copy(q).start()
+    own_copy.start()
     mates_moved.wait_recv()
     pltpu.make_async_copy(table_hbm, table, table_sem).wait()
 
@@ -304,10 +300,12 @@
             for i in range(cap):
                 own_rows[u, i : i + 1, :] = table[pl.ds(ids_own[t, 0, 2 * cap + i], 1), :]
 
-    for s in range(AHEAD):
+    def fetch_ahead(s, carry):
         fetch_mate(s)
-    for q in range(SIDE):
-        own_copy(q).wait()
+        return carry
+
+    lax.fori_loop(0, AHEAD, fetch_ahead, 0)
+    own_copy.wait()
     fetch_own(0)
 
     bag_iota = lax.broadcasted_iota(I32, (bags, 2 * cap), 0)
@@ -375,9 +373,7 @@
                 elif v and v != joined(o):
                     a_copy(t, p, v, near_recv.at[p, team]).start()
 
-    for s in range(groups):
-        pool(s)
-    for team in range(TEAMS):
+    def relay(team):
         planes = [o for o in PLANE if TEAM[PLACE[o]] == team]
         for p in range(3):
             lo, hi = CUT[p], CUT[p + 1]
@@ -386,6 +382,14 @@
                 t, far = SLOT[along(p, joined(o), o)], SLOT[along(p, FAR, o)]
                 a_out[t, lo:hi, :] = a_out[t, lo:hi, :] + a_in[far, lo:hi, :]
                 a_copy(t, p, joined(o), near_recv.at[p, team]).start()
+
+    for s in range(groups):
+        pool(s)
+        if s in EARLY:
+            relay(EARLY[s])
+    for team in range(TEAMS):
+        if team not in EARLY.values():
+            relay(team)
     for team in range(TEAMS):
         planes = [o for o in PLANE if TEAM[PLACE[o]] == team]
         for p in range(3):
@@ -500,7 +504,7 @@
             dma,
             dma,
             dma,
-            dma((SIDE,)),
+            dma,
             dma,
             dma((groups,)),
             dma,

time: 33.1 us -> 32.7 us (0.988)
  Pallas kernels: 32.3 us -> 31.9 us
    pallas_call x1, Pallas kernels: 31.5 us -> 31.2 us  [shards(): pl.pallas_call(functools.partial(kernel, dims), out_shape=(jax.ShapeDtype...]
where the time goes in v5:
time: 32.7 us; the launch traced here: 32.6 us
  Pallas kernels  31.9 us (98%)
  between operations  0.67 us (2%)
    pallas_call x1, Pallas kernels, shards(): pl.pallas_call(functools.partial(kernel, dims), out_shape=(jax.ShapeDtype...  31.2 us
    pallas_call x1, Pallas kernels, shards(): pl.pallas_call(interact, out_shape=(jax.ShapeDtypeStruct((samples, nt, wi...  0.77 us

profile of v5, /device:TPU:0, one launch (start us, length us, event | category | flops | bytes accessed | tf_op | source)
XLA Modules:
  0.0 32.6 jit_solution(10504338805795503749)
XLA Ops:
  0.6 0.0 copy-start.1
  0.6 0.0 copy-start
  0.7 31.2 %shard_map.86 = (f32[64,128]{1,0:T(8,128)S(1)}, f32[16,1024]{1,0:T(8,128)S(1)}) custom-call(s32[16,128]{1,0:T(8,128)} %index_hbm.1, s32[4,16]{1,0:T(4,128)} %bitcast.5, f32[32768,128]{1,0:T(8,128)} %bitcast.3, f32[16,128]{1,0:T(8,128)} %dense_ref.1, f32[128,1024]{1,0:T(8,128)} %wd_hbm.1, f32[1,1024]{1,0:T(1,128)} %bitcast.4), custom_call_target="tpu_custom_call" | custom-call | tf_op jit(solution)/shard_map/pallas_call | solution.py:475
  31.8 0.0 copy-done.1
  31.8 0.0 copy-done
  31.8 0.8 %shard_map.87 = (f32[16,4,128]{2,1,0:T(4,128)}, f32[16,1024]{1,0:T(8,128)}) custom-call(f32[64,128]{1,0:T(8,128)S(1)} %get-tuple-element.4.sums_ref, f32[16,1024]{1,0:T(8,128)S(1)} %get-tuple-element.5.start_ref, f32[16,128]{1,0:T(8,128)S(1)} %copy-done.1, f32[10,1024]{1,0:T(8,128)S(1)} %copy-done), custom_call_target="tpu_custom_call" | custom-call | tf_op jit(solution)/shard_map/pallas_call | solution.py:532
Async XLA Ops:
  0.6 31.2 %copy-start.1 = (f32[16,128]{1,0:T(8,128)S(1)}, f32[16,128]{1,0:T(8,128)}, u32[]{:S(2)}) copy-start(f32[16,128]{1,0:T(8,128)} %dense_ref.1) | copy-start | bytes 24580
  0.6 31.2 %copy-start = (f32[10,1024]{1,0:T(8,128)S(1)}, f32[10,1024]{1,0:T(8,128)}, u32[]{:S(2)}) copy-start(f32[10,1024]{1,0:T(8,128)} %wp_ref.1) | copy-start | bytes 122884

commit v6 on v5

--- a/solution.py
+++ b/solution.py
@@ -15,7 +15,9 @@
 CHIPS = SIDE**3
 CHUNKS = 8
 AHEAD = 5
-CUT = (0, 24, 48, 64)
+FIRST = (16, 24, 16, 24)
+SECOND = (40, 40, 48, 40)
+BAGS = 64
 FAR = SIDE // 2
 
 
@@ -51,6 +53,15 @@
 TEAM = [0] * 4 + [1] * 3 + [2] * 3 + [3] * 3 + [4] * 3
 TEAMS = 5
 EARLY = {13: 0, 15: 1}
+
+
+def span(p, o):
+    a, b = o
+    return ((0, FIRST[b]), (FIRST[b], SECOND[a]), (SECOND[a], BAGS))[p]
+
+
+def height(p, planes):
+    return sum(span(p, o)[1] - span(p, o)[0] for o in planes)
 
 
 def joined(o):
@@ -310,13 +321,15 @@
 
     bag_iota = lax.broadcasted_iota(I32, (bags, 2 * cap), 0)
 
-    def rows_of(p):
-        return pl.ds(CUT[p], CUT[p + 1] - CUT[p])
+    def rows_of(p, o):
+        lo, hi = span(p, o)
+        return pl.ds(lo, hi - lo)
 
     def a_copy(t, p, shift, recv):
+        rows = rows_of(p, others(ORDER[t], p))
         return pltpu.make_async_remote_copy(
-            src_ref=a_out.at[t, rows_of(p)],
-            dst_ref=a_in.at[t, rows_of(p)],
+            src_ref=a_out.at[t, rows],
+            dst_ref=a_in.at[t, rows],
             send_sem=a_send,
             recv_sem=recv,
             device_id=shifted(along(p, shift, (0, 0)), k),
@@ -325,18 +338,19 @@
 
     def b_copy(g, p):
         return pltpu.make_async_remote_copy(
-            src_ref=b_out.at[g, rows_of(p)],
-            dst_ref=b_in.at[g, rows_of(p)],
+            src_ref=b_out.at[g, rows_of(p, PLANE[g])],
+            dst_ref=b_in.at[g, rows_of(p, PLANE[g])],
             send_sem=b_send,
             recv_sem=b_recv,
             device_id=shifted(along(p, 0, PLANE[g]), k),
             device_id_type=MESH,
         )
 
-    def arrived(count, p, sem):
+    def arrived(count, sem):
+        tiles, some = pl.ds(0, count // 8), pl.ds(0, 8)
         pltpu.make_async_remote_copy(
-            src_ref=a_in.at[pl.ds(0, count), rows_of(p)],
-            dst_ref=a_in.at[pl.ds(0, count), rows_of(p)],
+            src_ref=a_in.at[tiles, some],
+            dst_ref=a_in.at[tiles, some],
             send_sem=a_send,
             recv_sem=sem,
             device_id=mate,
@@ -359,7 +373,8 @@
             a_out[t] = value
             for p in range(3):
                 if ORDER[t][p] == 0:
-                    a_in[t, CUT[p] : CUT[p + 1], :] = value[CUT[p] : CUT[p + 1]]
+                    lo, hi = span(p, others(ORDER[t], p))
+                    a_in[t, lo:hi, :] = value[lo:hi]
         if s + 1 < groups:
             fetch_own(s + 1)
         if s + AHEAD < groups:
@@ -376,9 +391,9 @@
     def relay(team):
         planes = [o for o in PLANE if TEAM[PLACE[o]] == team]
         for p in range(3):
-            lo, hi = CUT[p], CUT[p + 1]
-            arrived(len(planes), p, far_recv.at[p, team])
+            arrived(height(p, planes), far_recv.at[p, team])
             for o in planes:
+                lo, hi = span(p, o)
                 t, far = SLOT[along(p, joined(o), o)], SLOT[along(p, FAR, o)]
                 a_out[t, lo:hi, :] = a_out[t, lo:hi, :] + a_in[far, lo:hi, :]
                 a_copy(t, p, joined(o), near_recv.at[p, team]).start()
@@ -393,9 +408,9 @@
     for team in range(TEAMS):
         planes = [o for o in PLANE if TEAM[PLACE[o]] == team]
         for p in range(3):
-            lo, hi = CUT[p], CUT[p + 1]
-            arrived(2 * len(planes), p, near_recv.at[p, team])
+            arrived(2 * height(p, planes), near_recv.at[p, team])
             for o in planes:
+                lo, hi = span(p, o)
                 g = PLACE[o]
                 total = a_in[SLOT[along(p, 0, o)], lo:hi, :]
                 for v in (1, SIDE - 1):

time: 32.7 us -> 32.4 us (level)
  Pallas kernels: 31.9 us -> 31.5 us
    pallas_call x1, Pallas kernels: 31.2 us -> 30.7 us  [shards(): pl.pallas_call(functools.partial(kernel, dims), out_shape=(jax.ShapeDtype...]
where the time goes in v6:
time: 32.4 us; the launch traced here: 32.2 us
  Pallas kernels  31.5 us (97%)
  between operations  0.67 us (2%)
    pallas_call x1, Pallas kernels, shards(): pl.pallas_call(functools.partial(kernel, dims), out_shape=(jax.ShapeDtype...  30.7 us
    pallas_call x1, Pallas kernels, shards(): pl.pallas_call(interact, out_shape=(jax.ShapeDtypeStruct((samples, nt, wi...  0.77 us

profile of v6, /device:TPU:0, one launch (start us, length us, event | category | flops | bytes accessed | tf_op | source)
XLA Modules:
  0.0 32.2 jit_solution(9609220353929084473)
XLA Ops:
  0.6 0.0 copy-start.1
  0.6 0.0 copy-start
  0.7 30.7 %shard_map.86 = (f32[64,128]{1,0:T(8,128)S(1)}, f32[16,1024]{1,0:T(8,128)S(1)}) custom-call(s32[16,128]{1,0:T(8,128)} %index_hbm.1, s32[4,16]{1,0:T(4,128)} %bitcast.5, f32[32768,128]{1,0:T(8,128)} %bitcast.3, f32[16,128]{1,0:T(8,128)} %dense_ref.1, f32[128,1024]{1,0:T(8,128)} %wd_hbm.1, f32[1,1024]{1,0:T(1,128)} %bitcast.4), custom_call_target="tpu_custom_call" | custom-call | tf_op jit(solution)/shard_map/pallas_call | solution.py:490
  31.4 0.0 copy-done.1
  31.4 0.0 copy-done
  31.4 0.8 %shard_map.87 = (f32[16,4,128]{2,1,0:T(4,128)}, f32[16,1024]{1,0:T(8,128)}) custom-call(f32[64,128]{1,0:T(8,128)S(1)} %get-tuple-element.4.sums_ref, f32[16,1024]{1,0:T(8,128)S(1)} %get-tuple-element.5.start_ref, f32[16,128]{1,0:T(8,128)S(1)} %copy-done.1, f32[10,1024]{1,0:T(8,128)S(1)} %copy-done), custom_call_target="tpu_custom_call" | custom-call | tf_op jit(solution)/shard_map/pallas_call | solution.py:547
Async XLA Ops:
  0.6 30.8 %copy-start.1 = (f32[16,128]{1,0:T(8,128)S(1)}, f32[16,128]{1,0:T(8,128)}, u32[]{:S(2)}) copy-start(f32[16,128]{1,0:T(8,128)} %dense_ref.1) | copy-start | bytes 24580
  0.6 30.8 %copy-start = (f32[10,1024]{1,0:T(8,128)S(1)}, f32[10,1024]{1,0:T(8,128)}, u32[]{:S(2)}) copy-start(f32[10,1024]{1,0:T(8,128)} %wp_ref.1) | copy-start | bytes 122884

commit v7 on v6

--- a/solution.py
+++ b/solution.py
@@ -281,9 +281,10 @@
         device_id_type=MESH,
     )
 
-    own_copy = pltpu.make_async_copy(inbox, ids_own, own_sem)
-    boxes_moved.wait_recv()
-    own_copy.start()
+    def own_copy(q):
+        some = pl.ds(q * (CHIPS // SIDE), CHIPS // SIDE)
+        return pltpu.make_async_copy(inbox.at[some], ids_own.at[some], own_sem.at[q])
+
     mates_moved.wait_recv()
     pltpu.make_async_copy(table_hbm, table, table_sem).wait()
 
@@ -315,8 +316,12 @@
         fetch_mate(s)
         return carry
 
-    lax.fori_loop(0, AHEAD, fetch_ahead, 0)
-    own_copy.wait()
+    fetch_mate(0)
+    boxes_moved.wait_recv()
+    for q in range(SIDE):
+        own_copy(q).start()
+    lax.fori_loop(1, AHEAD, fetch_ahead, 0)
+    own_copy(0).wait()
     fetch_own(0)
 
     bag_iota = lax.broadcasted_iota(I32, (bags, 2 * cap), 0)
@@ -360,6 +365,8 @@
     groups = CHIPS // SIDE
 
     def pool(s):
+        if (s + 1) % SIDE == 0 and s + 1 < groups:
+            own_copy((s + 1) // SIDE).wait()
         rows_copy(s).wait_recv()
         slots = range(s * SIDE, (s + 1) * SIDE)
         for t in slots:
@@ -519,7 +526,7 @@
             dma,
             dma,
             dma,
-            dma,
+            dma((SIDE,)),
             dma,
             dma((groups,)),
             dma,

time: 32.4 us -> 32.2 us (level)
  Pallas kernels: 31.5 us -> 31 us
    pallas_call x1, Pallas kernels: 30.7 us -> 30.3 us  [shards(): pl.pallas_call(functools.partial(kernel, dims), out_shape=(jax.ShapeDtype...]
where the time goes in v7:
time: 32.2 us; the launch traced here: 31.7 us
  Pallas kernels  31 us (96%)
  between operations  0.67 us (2%)
    pallas_call x1, Pallas kernels, shards(): pl.pallas_call(functools.partial(kernel, dims), out_shape=(jax.ShapeDtype...  30.3 us
    pallas_call x1, Pallas kernels, shards(): pl.pallas_call(interact, out_shape=(jax.ShapeDtypeStruct((samples, nt, wi...  0.77 us

profile of v7, /device:TPU:0, one launch (start us, length us, event | category | flops | bytes accessed | tf_op | source)
XLA Modules:
  0.0 31.7 jit_solution(12686876699642482985)
XLA Ops:
  0.6 0.0 copy-start.1
  0.6 0.0 copy-start
  0.7 30.3 %shard_map.86 = (f32[64,128]{1,0:T(8,128)S(1)}, f32[16,1024]{1,0:T(8,128)S(1)}) custom-call(s32[16,128]{1,0:T(8,128)} %index_hbm.1, s32[4,16]{1,0:T(4,128)} %bitcast.5, f32[32768,128]{1,0:T(8,128)} %bitcast.3, f32[16,128]{1,0:T(8,128)} %dense_ref.1, f32[128,1024]{1,0:T(8,128)} %wd_hbm.1, f32[1,1024]{1,0:T(1,128)} %bitcast.4), custom_call_target="tpu_custom_call" | custom-call | tf_op jit(solution)/shard_map/pallas_call | solution.py:497
  30.9 0.0 copy-done.1
  30.9 0.0 copy-done
  31.0 0.8 %shard_map.87 = (f32[16,4,128]{2,1,0:T(4,128)}, f32[16,1024]{1,0:T(8,128)}) custom-call(f32[64,128]{1,0:T(8,128)S(1)} %get-tuple-element.4.sums_ref, f32[16,1024]{1,0:T(8,128)S(1)} %get-tuple-element.5.start_ref, f32[16,128]{1,0:T(8,128)S(1)} %copy-done.1, f32[10,1024]{1,0:T(8,128)S(1)} %copy-done), custom_call_target="tpu_custom_call" | custom-call | tf_op jit(solution)/shard_map/pallas_call | solution.py:554
Async XLA Ops:
  0.6 30.3 %copy-start.1 = (f32[16,128]{1,0:T(8,128)S(1)}, f32[16,128]{1,0:T(8,128)}, u32[]{:S(2)}) copy-start(f32[16,128]{1,0:T(8,128)} %dense_ref.1) | copy-start | bytes 24580
  0.6 30.3 %copy-start = (f32[10,1024]{1,0:T(8,128)S(1)}, f32[10,1024]{1,0:T(8,128)}, u32[]{:S(2)}) copy-start(f32[10,1024]{1,0:T(8,128)} %wp_ref.1) | copy-start | bytes 122884

commit v8 on v7

--- a/solution.py
+++ b/solution.py
@@ -15,8 +15,8 @@
 CHIPS = SIDE**3
 CHUNKS = 8
 AHEAD = 5
-FIRST = (16, 24, 16, 24)
-SECOND = (40, 40, 48, 40)
+FIRST = (24, 24, 16, 24)
+SECOND = (40, 48, 40, 48)
 BAGS = 64
 FAR = SIDE // 2
 

time: 32.2 us -> 32 us (level)
  no operation moved by 1% of the time
where the time goes in v8:
time: 32 us; the launch traced here: 31.7 us
  Pallas kernels  31 us (97%)
  between operations  0.67 us (2%)
    pallas_call x1, Pallas kernels, shards(): pl.pallas_call(functools.partial(kernel, dims), out_shape=(jax.ShapeDtype...  30.3 us
    pallas_call x1, Pallas kernels, shards(): pl.pallas_call(interact, out_shape=(jax.ShapeDtypeStruct((samples, nt, wi...  0.77 us

profile of v8, /device:TPU:0, one launch (start us, length us, event | category | flops | bytes accessed | tf_op | source)
XLA Modules:
  0.0 31.7 jit_solution(17768763439784696693)
XLA Ops:
  0.6 0.0 copy-start.1
  0.6 0.0 copy-start
  0.7 30.3 %shard_map.86 = (f32[64,128]{1,0:T(8,128)S(1)}, f32[16,1024]{1,0:T(8,128)S(1)}) custom-call(s32[16,128]{1,0:T(8,128)} %index_hbm.1, s32[4,16]{1,0:T(4,128)} %bitcast.5, f32[32768,128]{1,0:T(8,128)} %bitcast.3, f32[16,128]{1,0:T(8,128)} %dense_ref.1, f32[128,1024]{1,0:T(8,128)} %wd_hbm.1, f32[1,1024]{1,0:T(1,128)} %bitcast.4), custom_call_target="tpu_custom_call" | custom-call | tf_op jit(solution)/shard_map/pallas_call | solution.py:497
  30.9 0.0 copy-done.1
  30.9 0.0 copy-done
  30.9 0.8 %shard_map.87 = (f32[16,4,128]{2,1,0:T(4,128)}, f32[16,1024]{1,0:T(8,128)}) custom-call(f32[64,128]{1,0:T(8,128)S(1)} %get-tuple-element.4.sums_ref, f32[16,1024]{1,0:T(8,128)S(1)} %get-tuple-element.5.start_ref, f32[16,128]{1,0:T(8,128)S(1)} %copy-done.1, f32[10,1024]{1,0:T(8,128)S(1)} %copy-done), custom_call_target="tpu_custom_call" | custom-call | tf_op jit(solution)/shard_map/pallas_call | solution.py:554
Async XLA Ops:
  0.6 30.3 %copy-start.1 = (f32[16,128]{1,0:T(8,128)S(1)}, f32[16,128]{1,0:T(8,128)}, u32[]{:S(2)}) copy-start(f32[16,128]{1,0:T(8,128)} %dense_ref.1) | copy-start | bytes 24580
  0.6 30.3 %copy-start = (f32[10,1024]{1,0:T(8,128)S(1)}, f32[10,1024]{1,0:T(8,128)}, u32[]{:S(2)}) copy-start(f32[10,1024]{1,0:T(8,128)} %wp_ref.1) | copy-start | bytes 122884

commit v9 on v8

--- a/solution.py
+++ b/solution.py
@@ -14,7 +14,7 @@
 SIDE = 4
 CHIPS = SIDE**3
 CHUNKS = 8
-AHEAD = 5
+AHEAD = 6
 FIRST = (24, 24, 16, 24)
 SECOND = (40, 48, 40, 48)
 BAGS = 64

time: 32 us -> 32 us (level)
  no operation moved by 1% of the time
where the time goes in v9:
time: 32 us; the launch traced here: 31.8 us
  Pallas kernels  31.1 us (97%)
  between operations  0.67 us (2%)
    pallas_call x1, Pallas kernels, shards(): pl.pallas_call(functools.partial(kernel, dims), out_shape=(jax.ShapeDtype...  30.3 us
    pallas_call x1, Pallas kernels, shards(): pl.pallas_call(interact, out_shape=(jax.ShapeDtypeStruct((samples, nt, wi...  0.77 us

profile of v9, /device:TPU:0, one launch (start us, length us, event | category | flops | bytes accessed | tf_op | source)
XLA Modules:
  0.0 31.8 jit_solution(8976107514812423729)
XLA Ops:
  0.6 0.0 copy-start.1
  0.6 0.0 copy-start
  0.7 30.3 %shard_map.86 = (f32[64,128]{1,0:T(8,128)S(1)}, f32[16,1024]{1,0:T(8,128)S(1)}) custom-call(s32[16,128]{1,0:T(8,128)} %index_hbm.1, s32[4,16]{1,0:T(4,128)} %bitcast.5, f32[32768,128]{1,0:T(8,128)} %bitcast.3, f32[16,128]{1,0:T(8,128)} %dense_ref.1, f32[128,1024]{1,0:T(8,128)} %wd_hbm.1, f32[1,1024]{1,0:T(1,128)} %bitcast.4), custom_call_target="tpu_custom_call" | custom-call | tf_op jit(solution)/shard_map/pallas_call | solution.py:497
  31.0 0.0 copy-done.1
  31.0 0.0 copy-done
  31.0 0.8 %shard_map.87 = (f32[16,4,128]{2,1,0:T(4,128)}, f32[16,1024]{1,0:T(8,128)}) custom-call(f32[64,128]{1,0:T(8,128)S(1)} %get-tuple-element.4.sums_ref, f32[16,1024]{1,0:T(8,128)S(1)} %get-tuple-element.5.start_ref, f32[16,128]{1,0:T(8,128)S(1)} %copy-done.1, f32[10,1024]{1,0:T(8,128)S(1)} %copy-done), custom_call_target="tpu_custom_call" | custom-call | tf_op jit(solution)/shard_map/pallas_call | solution.py:554
Async XLA Ops:
  0.6 30.4 %copy-start.1 = (f32[16,128]{1,0:T(8,128)S(1)}, f32[16,128]{1,0:T(8,128)}, u32[]{:S(2)}) copy-start(f32[16,128]{1,0:T(8,128)} %dense_ref.1) | copy-start | bytes 24580
  0.6 30.4 %copy-start = (f32[10,1024]{1,0:T(8,128)S(1)}, f32[10,1024]{1,0:T(8,128)}, u32[]{:S(2)}) copy-start(f32[10,1024]{1,0:T(8,128)} %wp_ref.1) | copy-start | bytes 122884
